TPU v7x, 128 devices: a whole 4x4x4 slice. The times are simulated.
128 devices in a mesh: ops: 64 (over y, x, z), blk: 2 (over core).
Axes of the slice: x: 4, y: 4, z: 4, core: 2. Of those that a mesh axis runs over, the one named last changes fastest.
Arguments:
- operators_left: bfloat16 [4096, 256, 256], P('ops', None, 'blk'), may hold values from -16 to 16
- operators_right: bfloat16 [4096, 256, 256], P('ops'), may hold values from -0.00036621094 to 0.00036621094
- wavefunction: bfloat16 [256, 3, 256], P('blk', None, 'ops'), may hold values from -6 to 6
- rotation: bfloat16 [256, 128], replicated, may hold values from -0.375 to 0.375
- pair_count: int32 [64], P('ops'), may hold values from 16 to 64, as said below
- next_owner: int32 [4096, 1], P('ops'), may hold values from 0 to 63; in each aligned block of 64 rows (0 to 63, 64 to 127, ...) at most 2 rows name the same one
Outputs:
- sigma: float32 [256, 3, 256], P(('ops', 'blk'))
- renewed: bfloat16 [64, 128, 128, 128], P('ops', None, 'blk')
Inputs may be any that keep to these rules, and one draw needn't show every extreme that they name: Each owner's live pairs fill its first pair_count slots; at least one owner has all 64 slots live. `next_owner`: among the 64 slots of one owner, at most 2 name the same next owner.
All inputs are finite; a program needn't handle non-finite values.
Results may differ from a plain program's by a relative error of at most 0.0073.
Values may be sent and summed in bfloat16 or wider, within the bound.
No kernel may reach another device: no remote copies, remote signals or barrier semaphores. Data moves between devices by JAX's collectives and lax.ppermute only.
A program may use at most 128 MiB of HBM per device.

v0:
```python
import jax
import jax.numpy as jnp
from jax import lax
from jax.sharding import Mesh
from jax.sharding import PartitionSpec as P

OPS = ("ops_0", "ops_1", "ops_2")
OPS_BLK = ("ops_0", "ops_1", "ops_2", "blk")


def copy_for_each(shard, axis):
    copies = jnp.broadcast_to(shard, (lax.axis_size(axis), *shard.shape))
    return lax.all_to_all(copies, axis, split_axis=0, concat_axis=0, tiled=True)


def joined_along(blocks, dim):
    dims = list(blocks.shape[1:])
    dims[dim] *= blocks.shape[0]
    return jnp.moveaxis(blocks, 0, dim).reshape(dims)


def gather_directly(shard, axis, dim):
    blocks = copy_for_each(shard, axis)
    return joined_along(blocks, dim)


def in_blocks(shard, dim, length):
    before, after = (shard.shape[:dim], shard.shape[dim + 1 :])
    return jnp.moveaxis(shard.reshape(*before, length, -1, *after), dim, 0)


def sum_at_owner(shard, axis, dim):
    length = lax.axis_size(axis)
    blocks = lax.all_to_all(in_blocks(shard, dim, length), axis, 0, 0, tiled=True)
    return jnp.sum(blocks.astype(jnp.float32), axis=0)


def sum_by_axis(shard, axes, dim):
    far, near = axes
    own = sum_at_owner(in_blocks(shard, dim, lax.axis_size(far)), near, dim + 1)
    return jnp.sum(
        lax.all_to_all(own.astype(jnp.bfloat16), far, 0, 0, tiled=True).astype(jnp.float32), axis=0
    )


def over_slots(operation, operand, live_count, template):
    slot_total = template.shape[0]
    results = jax.vmap(operation)(operand)
    living = lax.iota(jnp.int32, slot_total) < live_count
    living = living.reshape((slot_total,) + (1,) * (results.ndim - 1))
    return jnp.where(living, results, jnp.zeros_like(results))


def per_device(operators_left, operators_right, wavefunction, rotation, pair_count, next_owner):
    slot_total = operators_left.shape[0]
    left_states = operators_left.shape[1]
    half_cols = operators_left.shape[2]
    right_states = operators_right.shape[1]
    vectors = wavefunction.shape[1]
    new_states = rotation.shape[1]
    live_count = pair_count[0]
    rows_half = gather_directly(wavefunction, OPS, 2)

    def right_apply(single_right):
        return jnp.einsum(
            "inr,sr->ins", rows_half, single_right, preferred_element_type=jnp.float32
        ).astype(jnp.bfloat16)

    products = over_slots(
        right_apply,
        operators_right,
        live_count,
        jnp.zeros((slot_total, half_cols, vectors, right_states), jnp.bfloat16),
    )
    products = products.reshape(slot_total, half_cols, vectors * right_states)
    own_rows = left_states // (lax.axis_size(OPS) * lax.axis_size("blk"))
    sigma_flat = sum_by_axis(
        jnp.einsum(
            "pij,pjn->in", operators_left, products, preferred_element_type=jnp.float32
        ).astype(jnp.bfloat16),
        (("ops_0", "ops_1", "ops_2"), "blk"),
        0,
    )
    sigma = sigma_flat.reshape(own_rows, vectors, right_states)
    new_half = new_states // lax.axis_size("blk")
    rot_rows = lax.dynamic_slice_in_dim(rotation, lax.axis_index("blk") * half_cols, half_cols, 0)

    def renew_partial(single_left):
        rotated = jnp.einsum(
            "ik,ij->kj", rotation, single_left, preferred_element_type=jnp.float32
        ).astype(jnp.bfloat16)
        return jnp.dot(rotated, rot_rows, preferred_element_type=jnp.float32)

    partials = over_slots(
        renew_partial,
        operators_left,
        live_count,
        jnp.zeros((slot_total, new_states, new_states), jnp.float32),
    )
    renewed = sum_at_owner(partials.astype(jnp.bfloat16), "blk", 1).astype(jnp.bfloat16)
    owners = lax.axis_size(OPS)
    capacity = max(2, 2 * slot_total // owners)
    targets = next_owner[:, 0]
    living = lax.iota(jnp.int32, slot_total) < live_count
    chosen = ((targets[:, None] == lax.iota(jnp.int32, owners)[None, :]) & living[:, None]).astype(
        jnp.int32
    )
    earlier = jnp.cumsum(chosen, axis=0) - chosen
    ranking = jnp.sum(earlier * chosen, axis=1)
    address = targets * capacity + ranking
    placing = (
        (address[None, :] == lax.iota(jnp.int32, owners * capacity)[:, None]) & living[None, :]
    ).astype(jnp.bfloat16)
    flat_blocks = renewed.reshape(slot_total, new_half * new_states)
    outgoing = jnp.dot(placing, flat_blocks, preferred_element_type=jnp.float32).astype(
        jnp.bfloat16
    )
    outgoing = outgoing.reshape(owners * capacity, new_half, new_states)
    incoming = lax.all_to_all(outgoing, OPS, split_axis=0, concat_axis=0, tiled=True)
    return (sigma, incoming[None])


def solution(mesh):
    split = Mesh(
        mesh.devices.reshape(4, 4, 4, mesh.shape["blk"]), ("ops_0", "ops_1", "ops_2", "blk")
    )
    placed = (
        P(OPS, None, "blk"),
        P(OPS, None, None),
        P("blk", None, OPS),
        P(),
        P(OPS),
        P(OPS, None),
    )
    return jax.shard_map(
        per_device,
        mesh=split,
        in_specs=placed,
        out_specs=(P(OPS_BLK, None, None), P(OPS, None, "blk", None)),
        check_vma=False,
    )
```

profile of v0, /device:TPU:0, one launch (start us, length us, event | category | flops | bytes accessed | tf_op | source)
XLA Modules:
  0.0 122.3 jit_solution(16824278560882605545)
XLA Ops:
  0.6 0.0 copy-start
  0.6 0.0 copy-start.1
  0.7 1.4 %broadcast_in_dim.34 = bf16[64,128,3,4]{1,3,2,0:T(4,128)(2,1)} broadcast(bf16[128,3,4]{0,2,1:T(4,128)(2,1)} %param.8), dimensions={1,2,3} | broadcast | bytes 199680 | tf_op jit(solution)/shard_map/broadcast_in_dim | solution.py:12
  2.1 11.5 %all-to-all-start = ((bf16[64,128,3,4]{1,3,2,0:T(4,128)(2,1)}), bf16[64,128,3,4]{1,3,2,0:T(4,128)(2,1)S(1)}, u32[]{:S(2)}, u32[]{:S(2)}) async-start(bf16[64,128,3,4]{1,3,2,0:T(4,128)(2,1)} %broadcast_in_dim.34), calls=%async_computation | async-start | bytes 393216 | tf_op jit(solution)/shard_map/all_to_all | solution.py:13
  14.3 0.0 copy-done
  14.3 3.5 %select_convert_fusion = bf16[128,64,128]{2,0,1:T(8,128)(2,1)S(1)} fusion(bf16[64,256,128]{2,1,0:T(8,128)(2,1)} %param.6, pred[64]{0:T(512)(128)(4,1)S(1)} %iota_compare_fusion.2, bf16[256,128]{1,0:T(8,128)(2,1)S(1)} %copy-done, s32[]{:T(128)S(6)} %select_n.17), kind=kOutput, calls=%fused_computation.4 | convolution fusion | flops 808452096 | bytes 6390276 | tf_op jit(solution)/shard_map/vmap()/dot_general | solution.py:92
  17.8 0.0 copy-done.1
  17.8 0.1 fusion.20
  17.9 1.5 %copy.68 = bf16[64,2,64,128]{3,2,0,1:T(8,128)(2,1)} copy(bf16[64,2,64,128]{3,2,1,0:T(8,128)(2,1)S(1)} %bitcast.57) | data formatting | bytes 4194304 | tf_op jit(solution)/shard_map/reshape | solution.py:29
  19.4 0.1 reduce_window_sum.11
  19.5 0.2 select_reduce_fusion
  19.7 4.2 %all-to-all-done = bf16[64,128,3,4]{1,3,2,0:T(4,128)(2,1)S(1)} async-done(((bf16[64,128,3,4]{1,3,2,0:T(4,128)(2,1)}), bf16[64,128,3,4]{1,3,2,0:T(4,128)(2,1)S(1)}, u32[]{:S(2)}, u32[]{:S(2)}) %all-to-all-start) | async-done | bytes 196640 | tf_op jit(solution)/shard_map/all_to_all | solution.py:13
  23.9 0.1 copy.44
  23.9 9.9 %select_bitcast_fusion = bf16[64,128,3,256]{3,1,0,2:T(8,128)(2,1)} fusion(pred[64]{0:T(512)(128)(4,1)S(1)} %iota_compare_fusion.2, bf16[128,3,256,1]{0,2,3,1:T(8,128)(2,1)S(1)} %bitcast.61, bf16[64,256,256]{2,1,0:T(8,128)(2,1)} %param.7), kind=kOutput, calls=%fused_computation | convolution fusion | flops 3233808384 | bytes 21168192 | tf_op jit(solution)/shard_map/vmap(inr,sr->ins)/dot_general | solution.py:65
  33.8 16.7 %copy.46 = bf16[64,128,3,256]{1,3,2,0:T(8,128)(2,1)} copy(bf16[64,128,3,256]{3,1,0,2:T(8,128)(2,1)} %select_bitcast_fusion) | data formatting | bytes 25165824 | tf_op jit(solution)/shard_map/jit(_where)/select_n | solution.py:51
  50.5 9.2 %fusion.9 = bf16[256,768]{1,0:T(8,128)(2,1)S(1)} fusion(bf16[64,128,768]{1,2,0:T(8,128)(2,1)} %bitcast.55, bf16[64,256,128]{2,1,0:T(8,128)(2,1)} %param.6), kind=kOutput, calls=%fused_computation.11 | convolution fusion | flops 3221422080 | bytes 17170432 | tf_op jit(solution)/shard_map/pij,pjn->in/dot_general | solution.py:78
  59.7 0.1 reshape_reshape.3
  59.8 0.3 copy.69
  60.1 4.0 %all_to_all.25 = bf16[2,64,2,768]{3,2,1,0:T(2,128)(2,1)S(1)} all-to-all(bf16[2,64,2,768]{3,2,1,0:T(2,128)(2,1)S(1)} %bitcast.59), channel_id=1, replica_groups=mesh['ops_0'=4,'ops_1'=4,'ops_2'=4,'blk'=2] {'blk'}, dimensions={0} | all-to-all | bytes 786432 | tf_op jit(solution)/shard_map/all_to_all | solution.py:34
  64.2 3.8 %all-to-all-start.3 = ((bf16[2,64,64,128]{3,2,1,0:T(8,128)(2,1)}), bf16[2,64,64,128]{3,2,1,0:T(8,128)(2,1)S(1)}, u32[]{:S(2)}, u32[]{:S(2)}) async-start(bf16[2,64,64,128]{3,2,1,0:T(8,128)(2,1)} %bitcast.52), calls=%async_computation.3 | async-start | bytes 4194304 | tf_op jit(solution)/shard_map/all_to_all | solution.py:34
  67.9 1.5 %reduce_sum.42 = bf16[64,2,768]{2,1,0:T(2,128)(2,1)} reduce(bf16[2,64,2,768]{3,2,1,0:T(2,128)(2,1)S(1)} %all_to_all.25, bf16[]{:T(256)} %constant.7.clone.1), dimensions={0}, to_apply=%region_0.1 | reduce | flops 98304 | bytes 589826 | tf_op jit(solution)/shard_map/reduce_sum | solution.py:35
  69.4 1.4 %all-to-all-done.3 = bf16[2,64,64,128]{3,2,1,0:T(8,128)(2,1)S(1)} async-done(((bf16[2,64,64,128]{3,2,1,0:T(8,128)(2,1)}), bf16[2,64,64,128]{3,2,1,0:T(8,128)(2,1)S(1)}, u32[]{:S(2)}, u32[]{:S(2)}) %all-to-all-start.3) | async-done | bytes 2097184 | tf_op jit(solution)/shard_map/all_to_all | solution.py:34
  70.8 6.3 %all-to-all-start.2 = ((bf16[64,2,768]{2,1,0:T(2,128)(2,1)}), bf16[64,2,768]{2,1,0:T(2,128)(2,1)S(1)}, u32[]{:S(2)}, u32[]{:S(2)}) async-start(bf16[64,2,768]{2,1,0:T(2,128)(2,1)} %reduce_sum.42), calls=%async_computation.2 | async-start | bytes 393216 | tf_op jit(solution)/shard_map/all_to_all | solution.py:42
  77.2 0.6 reduce_sum.45
  77.7 0.9 fusion.7
  78.7 1.9 %copy.60 = bf16[16,8,64,128]{3,2,1,0:T(8,128)(2,1)} copy(bf16[16,8,64,128]{3,1,2,0:T(8,128)(2,1)S(1)} %fusion.7) | data formatting | bytes 4194304
  80.6 6.6 %all-to-all-done.2 = bf16[64,2,768]{2,1,0:T(2,128)(2,1)S(1)} async-done(((bf16[64,2,768]{2,1,0:T(2,128)(2,1)}), bf16[64,2,768]{2,1,0:T(2,128)(2,1)S(1)}, u32[]{:S(2)}, u32[]{:S(2)}) %all-to-all-start.2) | async-done | bytes 196640 | tf_op jit(solution)/shard_map/all_to_all | solution.py:42
  87.2 4.9 %all-to-all-start.4 = ((bf16[128,64,128]{2,1,0:T(8,128)(2,1)}), bf16[128,64,128]{2,1,0:T(8,128)(2,1)S(1)}, u32[]{:S(2)}, u32[]{:S(2)}) async-start(bf16[128,64,128]{2,1,0:T(8,128)(2,1)} %bitcast.25), calls=%async_computation.4 | async-start | bytes 4194304 | tf_op jit(solution)/shard_map/all_to_all | solution.py:119
  92.1 0.6 convert_reduce_fusion
  92.8 28.2 %all-to-all-done.4 = bf16[128,64,128]{2,1,0:T(8,128)(2,1)S(1)} async-done(((bf16[128,64,128]{2,1,0:T(8,128)(2,1)}), bf16[128,64,128]{2,1,0:T(8,128)(2,1)S(1)}, u32[]{:S(2)}, u32[]{:S(2)}) %all-to-all-start.4) | async-done | bytes 2097184 | tf_op jit(solution)/shard_map/all_to_all | solution.py:119
  121.0 1.3 %copy.72 = bf16[1,128,64,128]{3,2,1,0:T(8,128)(2,1)} copy(bf16[1,128,64,128]{3,2,1,0:T(8,128)(2,1)S(1)} %bitcast.56) | data formatting | bytes 4194304
  (2 shorter events, 0.0 us)
Async XLA Ops:
  0.6 13.7 %copy-start = (bf16[256,128]{1,0:T(8,128)(2,1)S(1)}, bf16[256,128]{1,0:T(8,128)(2,1)}, u32[]{:S(2)}) copy-start(bf16[256,128]{1,0:T(8,128)(2,1)} %param.9) | copy-start | bytes 196612
  0.6 17.2 %copy-start.1 = (s32[64,1]{0,1:T(1,128)S(1)}, s32[64,1]{0,1:T(1,128)}, u32[]{:S(2)}) copy-start(s32[64,1]{0,1:T(1,128)} %param.11) | copy-start | bytes 772
  2.1 21.8 %all-to-all-start = ((bf16[64,128,3,4]{1,3,2,0:T(4,128)(2,1)}), bf16[64,128,3,4]{1,3,2,0:T(4,128)(2,1)S(1)}, u32[]{:S(2)}, u32[]{:S(2)}) async-start(bf16[64,128,3,4]{1,3,2,0:T(4,128)(2,1)} %broadcast_in_dim.34), calls=%async_computation | async-start | bytes 393216 | tf_op jit(solution)/shard_map/all_to_all | solution.py:13
  64.2 6.6 %all-to-all-start.3 = ((bf16[2,64,64,128]{3,2,1,0:T(8,128)(2,1)}), bf16[2,64,64,128]{3,2,1,0:T(8,128)(2,1)S(1)}, u32[]{:S(2)}, u32[]{:S(2)}) async-start(bf16[2,64,64,128]{3,2,1,0:T(8,128)(2,1)} %bitcast.52), calls=%async_computation.3 | async-start | bytes 4194304 | tf_op jit(solution)/shard_map/all_to_all | solution.py:34
  70.8 16.4 %all-to-all-start.2 = ((bf16[64,2,768]{2,1,0:T(2,128)(2,1)}), bf16[64,2,768]{2,1,0:T(2,128)(2,1)S(1)}, u32[]{:S(2)}, u32[]{:S(2)}) async-start(bf16[64,2,768]{2,1,0:T(2,128)(2,1)} %reduce_sum.42), calls=%async_computation.2 | async-start | bytes 393216 | tf_op jit(solution)/shard_map/all_to_all | solution.py:42
  87.2 33.8 %all-to-all-start.4 = ((bf16[128,64,128]{2,1,0:T(8,128)(2,1)}), bf16[128,64,128]{2,1,0:T(8,128)(2,1)S(1)}, u32[]{:S(2)}, u32[]{:S(2)}) async-start(bf16[128,64,128]{2,1,0:T(8,128)(2,1)} %bitcast.25), calls=%async_computation.4 | async-start | bytes 4194304 | tf_op jit(solution)/shard_map/all_to_all | solution.py:119
where the time goes:
time: 123 us; the launch traced here: 122 us
  waiting for transfers between devices  40.3 us (33%)
  starting transfers between devices  26.6 us (22%)
  matrix products  23.5 us (19%)
  local copies, waits for them, and re-layouts  23.4 us (19%)
  blocking collectives  4.05 us (3%)
  other arithmetic  3.06 us (2%)
  between operations  1.43 us (1%)
    all_to_all x1, waiting for transfers between devices, per_device(): lax.all_to_all(outgoing, OPS, split_axis=0, concat_axis=0, tiled=True)  28.2 us
    select_n x1, local copies, waits for them, and re-layouts, over_slots(): return jnp.where(living, results, jnp.zeros_like(results))  16.7 us
    all_to_all x1, starting transfers between devices, copy_for_each(): return lax.all_to_all(copies, axis, split_axis=0, concat_axis=0, tiled=True)  11.5 us
    dot_general x1, matrix products, right_apply(): jnp.einsum('inr,sr->ins', rows_half, single_right, preferred_element_type...  9.88 us
    dot_general x1, matrix products, per_device(): jnp.einsum('pij,pjn->in', operators_left, products, preferred_element_typ...  9.2 us
    all_to_all x1, waiting for transfers between devices, sum_by_axis(): lax.all_to_all(own.astype(jnp.bfloat16), far, 0, 0, tiled=True)  6.62 us
    all_to_all x1, starting transfers between devices, sum_by_axis(): lax.all_to_all(own.astype(jnp.bfloat16), far, 0, 0, tiled=True)  6.34 us
    all_to_all x1, starting transfers between devices, per_device(): lax.all_to_all(outgoing, OPS, split_axis=0, concat_axis=0, tiled=True)  4.93 us
  transfers between devices with their start and end apart: 4, of which 4 were waited for; matrix products, arithmetic and copies ran while one was open for 9% of the time, Pallas kernels for 0%

commit v1 on v0

v1 whole, which is shorter than its diff:
```python
import jax
import jax.numpy as jnp
from jax import lax
from jax.experimental import pallas as pl
from jax.experimental.pallas import tpu as pltpu
from jax.sharding import Mesh
from jax.sharding import PartitionSpec as P


OPS = ("ops_0", "ops_1", "ops_2")
ALL = ("ops_0", "ops_1", "ops_2", "blk")
GROUP = 8
MIB = 1 << 20
LANES = 128


def rotate_kernel(side_ref, left_ref, rot_ref, keep_ref, send_ref, lefts, turned, arrived):
    slots, half, width = keep_ref.shape
    groups = slots // GROUP

    def fetch(g):
        part = pl.ds(g * GROUP, GROUP)
        return pltpu.make_async_copy(left_ref.at[part], lefts.at[part], arrived.at[g])

    for g in range(groups):
        fetch(g).start()
    own_low = side_ref[0] == 0
    turned[...] = rot_ref[...].T
    rot = turned[...]
    for g in range(groups):
        fetch(g).wait()
        for p in range(g * GROUP, (g + 1) * GROUP, 2):
            both = jnp.concatenate([lefts[p], lefts[p + 1]], axis=1)
            rotated = jnp.dot(rot, both, preferred_element_type=jnp.float32).astype(jnp.bfloat16)
            low, high = rotated[:half], rotated[half:]
            keep = jnp.where(own_low, low, high)
            send = jnp.where(own_low, high, low)
            for q in range(2):
                keep_ref[p + q] = keep[:, q * width : (q + 1) * width]
                send_ref[p + q] = send[:, q * width : (q + 1) * width]


def rotate_left(side, operators_left, rotation):
    slots, rows, cols = operators_left.shape
    new = rotation.shape[1]
    half = jax.ShapeDtypeStruct((slots, new // 2, cols), jnp.bfloat16)
    vmem = pl.BlockSpec(memory_space=pltpu.VMEM)
    return pl.pallas_call(
        rotate_kernel,
        in_specs=[
            pl.BlockSpec(memory_space=pltpu.SMEM),
            pl.BlockSpec(memory_space=pltpu.HBM),
            vmem,
        ],
        out_specs=[vmem, vmem],
        out_shape=[half, half],
        scratch_shapes=[
            pltpu.VMEM((slots, rows, cols), jnp.bfloat16),
            pltpu.VMEM((new, rows), jnp.bfloat16),
            pltpu.SemaphoreType.DMA((slots // GROUP,)),
        ],
        compiler_params=pltpu.CompilerParams(vmem_limit_bytes=50 * MIB),
        cost_estimate=pl.CostEstimate(
            flops=2 * slots * rows * cols * new,
            bytes_accessed=2 * slots * cols * (rows + new),
            transcendentals=0,
        ),
        name="rotate_left",
    )(side, operators_left, rotation)


def renew_kernel(side_ref, count_ref, place_ref, keep_ref, other_ref, rot_ref, out_ref):
    slots, half, width = keep_ref.shape
    live = count_ref[0]
    own_low = side_ref[0] == 0
    top, bottom = rot_ref[:width], rot_ref[width:]
    rot_own = jnp.where(own_low, top, bottom)
    rot_far = jnp.where(own_low, bottom, top)
    rot = jnp.concatenate([rot_own, rot_far], axis=0)
    out_ref[...] = jnp.zeros_like(out_ref)
    for first in range(slots - GROUP, -1, -GROUP):
        w = jnp.concatenate(
            [keep_ref[first : first + GROUP], other_ref[first : first + GROUP]], axis=2
        ).reshape(GROUP * half, 2 * width)
        b = jnp.dot(w, rot, preferred_element_type=jnp.float32).astype(jnp.bfloat16)
        for q in range(GROUP - 1, -1, -1):
            block = b[q * half : (q + 1) * half]
            alive = first + q < live
            out_ref[jnp.where(alive, place_ref[first + q], 0)] = jnp.where(
                alive, block, jnp.zeros_like(block)
            )


def renew(side, count, places, keep, other, rotation, total):
    slots, half, width = keep.shape
    new = rotation.shape[1]
    smem = pl.BlockSpec(memory_space=pltpu.SMEM)
    vmem = pl.BlockSpec(memory_space=pltpu.VMEM)
    return pl.pallas_call(
        renew_kernel,
        in_specs=[smem, smem, smem, vmem, vmem, vmem],
        out_specs=vmem,
        out_shape=jax.ShapeDtypeStruct((total, half, new), jnp.bfloat16),
        cost_estimate=pl.CostEstimate(
            flops=2 * slots * half * 2 * width * new,
            bytes_accessed=2 * (2 * slots + total) * half * new,
            transcendentals=0,
        ),
        compiler_params=pltpu.CompilerParams(vmem_limit_bytes=12 * MIB),
        name="renew",
    )(side, count, places, keep, other, rotation)


def sigma_kernel(
    side_ref,
    count_ref,
    wave_ref,
    left_ref,
    right_ref,
    keep_ref,
    send_ref,
    lefts,
    rights,
    total,
    arrived,
):
    slots, rows, cols = lefts.shape
    right = rights.shape[1]
    vectors = wave_ref.shape[0] // cols
    groups = slots // GROUP
    live = count_ref[0]

    def fetch(g):
        part = pl.ds(g * GROUP, GROUP)
        return (
            pltpu.make_async_copy(right_ref.at[part], rights.at[part], arrived.at[0, g]),
            pltpu.make_async_copy(left_ref.at[part], lefts.at[part], arrived.at[1, g]),
        )

    for g in range(groups):
        for copy in fetch(g):
            copy.start()
    total[...] = jnp.zeros_like(total)

    def step(g, carry):
        for copy in fetch(g):
            copy.wait()

        @pl.when(g * GROUP < live)
        def _():
            wave = wave_ref[...]
            alive, products = [], []
            for p in range(GROUP):
                at = g * GROUP + p
                product = lax.dot_general(
                    wave, rights[at], (((1,), (1,)), ((), ())), preferred_element_type=jnp.float32
                ).astype(jnp.bfloat16)
                products.append(product)
                left = lefts[at]
                alive.append(jnp.where(at < live, left, jnp.zeros_like(left)))
            left = jnp.concatenate(alive, axis=1)
            for n in range(vectors):
                stacked = jnp.concatenate([z[n * cols : (n + 1) * cols] for z in products], axis=0)
                term = jnp.dot(left, stacked, preferred_element_type=jnp.float32)
                for c in range(right // LANES):
                    total[n * (right // LANES) + c] += term[:, c * LANES : (c + 1) * LANES]

        return carry

    lax.fori_loop(0, groups, step, 0)
    ring = keep_ref.shape[0]
    span = rows // keep_ref.shape[2]
    side = side_ref[0]
    for z in range(ring):
        for u in range(2):
            at = z * (span // ring) + u
            for c in range(total.shape[0]):
                lanes = slice(c * LANES, (c + 1) * LANES)
                mine = total[c, pl.ds(at + 2 * side, keep_ref.shape[2], stride=span)]
                theirs = total[c, pl.ds(at + 2 - 2 * side, keep_ref.shape[2], stride=span)]
                keep_ref[z, u, :, lanes] = mine
                send_ref[z, u, :, lanes] = theirs.astype(send_ref.dtype)


def apply_pairs(side, count, wave, operators_left, operators_right):
    slots, rows, cols = operators_left.shape
    right = operators_right.shape[1]
    vectors = wave.shape[0] // cols
    part = (4, 2, rows // 16, vectors * right)
    smem = pl.BlockSpec(memory_space=pltpu.SMEM)
    vmem = pl.BlockSpec(memory_space=pltpu.VMEM)
    hbm = pl.BlockSpec(memory_space=pltpu.HBM)
    flops = 2 * slots * (wave.shape[0] * right * right + rows * cols * vectors * right)
    return pl.pallas_call(
        sigma_kernel,
        in_specs=[smem, smem, vmem, hbm, hbm],
        out_specs=[vmem, vmem],
        out_shape=[
            jax.ShapeDtypeStruct(part, jnp.float32),
            jax.ShapeDtypeStruct(part, jnp.bfloat16),
        ],
        scratch_shapes=[
            pltpu.VMEM((slots, rows, cols), jnp.bfloat16),
            pltpu.VMEM((slots, right, right), jnp.bfloat16),
            pltpu.VMEM((vectors * right // LANES, rows, LANES), jnp.float32),
            pltpu.SemaphoreType.DMA((2, slots // GROUP)),
        ],
        cost_estimate=pl.CostEstimate(
            flops=flops,
            bytes_accessed=2 * slots * (rows * cols + right * right),
            transcendentals=0,
        ),
        compiler_params=pltpu.CompilerParams(vmem_limit_bytes=50 * MIB),
        name="apply_pairs",
    )(side, count, wave, operators_left, operators_right)


def store_kernel(in_ref, out_ref, done):
    copy = pltpu.make_async_copy(in_ref, out_ref, done)
    copy.start()
    copy.wait()


def store(x):
    return pl.pallas_call(
        store_kernel,
        in_specs=[pl.BlockSpec(memory_space=pltpu.VMEM)],
        out_specs=pl.BlockSpec(memory_space=pltpu.HBM),
        out_shape=jax.ShapeDtypeStruct(x.shape, x.dtype),
        scratch_shapes=[pltpu.SemaphoreType.DMA],
        cost_estimate=pl.CostEstimate(flops=1 << 22, bytes_accessed=4 * x.size, transcendentals=0),
        compiler_params=pltpu.CompilerParams(vmem_limit_bytes=8 * MIB),
        name="store",
    )(x)


def own_share(blocks, axis):
    size = lax.axis_size(axis)
    me = lax.axis_index(axis)
    parts = []
    for k in range(1, size):
        block = lax.dynamic_index_in_dim(blocks, (me + k) % size, 0, keepdims=False)
        hop = [(i, (i + k) % size) for i in range(size)]
        parts.append(lax.ppermute(block.astype(jnp.bfloat16), axis, hop))
    total = lax.dynamic_index_in_dim(blocks, me, 0, keepdims=False)
    for part in parts:
        total = total + part.astype(jnp.float32)
    return total


def gather_wave(wavefunction):
    cols, vectors, own = wavefunction.shape
    shard = jnp.transpose(wavefunction, (1, 2, 0))
    owners = lax.axis_size(OPS)
    blocks = lax.all_to_all(
        jnp.broadcast_to(shard, (owners, *shard.shape)), OPS, 0, 0, tiled=True
    )
    return jnp.transpose(blocks, (1, 3, 0, 2)).reshape(vectors * cols, owners * own)


def per_device(operators_left, operators_right, wavefunction, rotation, pair_count, next_owner):
    slots, left_states, _ = operators_left.shape
    right_states = operators_right.shape[1]
    vectors = wavefunction.shape[1]
    owners = lax.axis_size(OPS)
    capacity = max(2, 2 * slots // owners)
    side = lax.axis_index("blk").astype(jnp.int32).reshape(1)
    targets = next_owner[:, 0]
    order = lax.iota(jnp.int32, slots)
    same = (targets[:, None] == targets[None, :]) & (order[None, :] < order[:, None])
    places = targets * capacity + jnp.sum(same.astype(jnp.int32), axis=1)

    keep, send = rotate_left(side, operators_left, rotation)
    other = lax.ppermute(send, "blk", [(0, 1), (1, 0)])
    wave = gather_wave(wavefunction)
    outgoing = renew(side, pair_count, places, keep, other, rotation, owners * capacity)
    incoming = lax.all_to_all(outgoing, OPS, split_axis=0, concat_axis=0, tiled=True)
    mine, theirs = apply_pairs(side, pair_count, wave, operators_left, operators_right)
    got = lax.ppermute(theirs, "blk", [(0, 1), (1, 0)])
    mine = own_share(mine + got.astype(jnp.float32), "ops_2")
    parts = jnp.transpose(mine.astype(jnp.bfloat16), (1, 0, 2))
    parts = lax.all_to_all(parts, ("ops_0", "ops_1"), 0, 0, tiled=True)
    renewed = store(incoming)
    sigma = jnp.sum(parts.astype(jnp.float32), axis=0)
    sigma = sigma.reshape(left_states // (2 * owners), vectors, right_states)
    return (sigma, renewed[None])


def solution(mesh):
    split = Mesh(mesh.devices.reshape(4, 4, 4, mesh.shape["blk"]), ALL)
    placed = (
        P(OPS, None, "blk"),
        P(OPS, None, None),
        P("blk", None, OPS),
        P(),
        P(OPS),
        P(OPS, None),
    )
    return jax.shard_map(
        per_device,
        mesh=split,
        in_specs=placed,
        out_specs=(P(ALL, None, None), P(OPS, None, "blk", None)),
        check_vma=False,
    )
```

time: 123 us -> 91.8 us (0.75)
  matrix products: 23.5 us -> 0 us
  local copies, waits for them, and re-layouts: 23.4 us -> 2.39 us
  Pallas kernels: 0 us -> 13.3 us
  waiting for transfers between devices: 40.3 us -> 44.7 us
  blocking collectives: 4.05 us -> 0 us
  other arithmetic: 3.06 us -> 0.89 us
  starting transfers between devices: 26.6 us -> 28.7 us
    dot_general x4 -> x0, matrix products: 23.5 us -> none  [the longest x1 9.88 us: right_apply(): jnp.einsum('inr,sr->ins', rows_half, single_right, preferred_element_type...]
    select_n x1 -> x0, local copies, waits for them, and re-layouts: 16.7 us -> none  [over_slots(): return jnp.where(living, results, jnp.zeros_like(results))]
    pallas_call x0 -> x4, Pallas kernels: none -> 13.3 us  [the longest x1 5.17 us: apply_pairs(): pl.pallas_call(sigma_kernel, in_specs=[smem, smem, vmem, hbm, hbm], out_s...]
    ppermute x0 -> x5, starting transfers between devices: none -> 6.38 us  [the longest x3 5.73 us: own_share(): parts.append(lax.ppermute(block.astype(jnp.bfloat16), axis, hop))]
    all_to_all x1 -> x0, blocking collectives: 4.05 us -> none  [sum_at_owner(): lax.all_to_all(in_blocks(shard, dim, length), axis, 0, 0, tiled=True)]
    ppermute x0 -> x5, waiting for transfers between devices: none -> 4.04 us  [the longest x3 4.03 us: own_share(): parts.append(lax.ppermute(block.astype(jnp.bfloat16), axis, hop))]
    all_to_all x3 -> x2, starting transfers between devices: 21.6 us -> 17.6 us  [the longest x1 11.5 us: gather_wave(): lax.all_to_all(jnp.broadcast_to(shard, (owners, *shard.shape)), OPS, 0, 0...]
    unnamed x6 -> x5, local copies, waits for them, and re-layouts: 3.25 us -> 0.04 us
  transfers between devices with their start and end apart: 4 -> 8, of which waited for: 4 -> 5; matrix products, arithmetic and copies ran while one was open for 9% -> 2% of each run, Pallas kernels for 0% -> 7%
where the time goes in v1:
time: 91.8 us; the launch traced here: 91.5 us
  waiting for transfers between devices  44.7 us (49%)
  starting transfers between devices  28.7 us (31%)
  Pallas kernels  13.3 us (14%)
  local copies, waits for them, and re-layouts  2.39 us (3%)
  between operations  1.41 us (2%)
    all_to_all x1, waiting for transfers between devices, per_device(): lax.all_to_all(outgoing, OPS, split_axis=0, concat_axis=0, tiled=True)  26.3 us
    all_to_all x1, starting transfers between devices, gather_wave(): lax.all_to_all(jnp.broadcast_to(shard, (owners, *shard.shape)), OPS, 0, 0...  11.5 us
    all_to_all x1, waiting for transfers between devices, gather_wave(): lax.all_to_all(jnp.broadcast_to(shard, (owners, *shard.shape)), OPS, 0, 0...  9.58 us
    all_to_all x1, starting transfers between devices, per_device(): parts = lax.all_to_all(parts, ('ops_0', 'ops_1'), 0, 0, tiled=True)  6.1 us
    ppermute x3, starting transfers between devices, own_share(): parts.append(lax.ppermute(block.astype(jnp.bfloat16), axis, hop))  5.73 us
    pallas_call x1, Pallas kernels, apply_pairs(): pl.pallas_call(sigma_kernel, in_specs=[smem, smem, vmem, hbm, hbm], out_s...  5.17 us
    all_to_all x1, waiting for transfers between devices, per_device(): parts = lax.all_to_all(parts, ('ops_0', 'ops_1'), 0, 0, tiled=True)  4.77 us
    all_to_all x1, starting transfers between devices, per_device(): lax.all_to_all(outgoing, OPS, split_axis=0, concat_axis=0, tiled=True)  4.69 us
  transfers between devices with their start and end apart: 8, of which 5 were waited for; matrix products, arithmetic and copies ran while one was open for 2% of the time, Pallas kernels for 7%

profile of v1, /device:TPU:0, one launch (start us, length us, event | category | flops | bytes accessed | tf_op | source)
XLA Modules:
  0.0 91.5 jit_solution(15303600340502042963)
XLA Ops:
  0.6 1.4 %broadcast_in_dim.8 = bf16[64,3,4,128]{3,2,1,0:T(4,128)(2,1)} broadcast(bf16[3,4,128]{2,1,0:T(4,128)(2,1)} %bitcast.37), dimensions={1,2,3} | broadcast | bytes 199680 | tf_op jit(solution)/shard_map/broadcast_in_dim | solution.py:256
  2.0 11.5 %all-to-all-start = ((bf16[64,3,4,128]{3,2,1,0:T(4,128)(2,1)}), bf16[64,3,4,128]{3,2,1,0:T(4,128)(2,1)S(1)}, u32[]{:S(2)}, u32[]{:S(2)}) async-start(bf16[64,3,4,128]{3,2,1,0:T(4,128)(2,1)} %broadcast_in_dim.8), calls=%async_computation | async-start | bytes 393216 | tf_op jit(solution)/shard_map/all_to_all | solution.py:255
  14.2 9.6 %all-to-all-done = bf16[64,3,4,128]{3,2,1,0:T(4,128)(2,1)S(1)} async-done(((bf16[64,3,4,128]{3,2,1,0:T(4,128)(2,1)}), bf16[64,3,4,128]{3,2,1,0:T(4,128)(2,1)S(1)}, u32[]{:S(2)}, u32[]{:S(2)}) %all-to-all-start) | async-done | bytes 196640 | tf_op jit(solution)/shard_map/all_to_all | solution.py:255
  23.8 0.1 copy.14
  24.0 0.1 copy.15.wave_ref
  24.1 0.0 copy-start
  24.1 5.2 %apply_pairs.1 = (f32[4,2,16,768]{3,2,1,0:T(8,128)S(1)}, bf16[4,2,16,768]{3,2,1,0:T(8,128)(2,1)S(1)}) custom-call(s32[1]{0:T(128)} %bitcast.side_ref, s32[1]{0:T(128)S(6)} %copy.20.count_ref, bf16[384,256]{1,0:T(8,128)(2,1)S(1)} %copy.15.wave_ref, bf16[64,256,128]{2,1,0:T(8,128)(2,1)} %left_ref.3, bf16[64,256,256]{2,1,0:T(8,128)(2,1)} %right_ref.1), custom_call_target="tpu_custom_call" | custom-call | flops 6442450944 | bytes 12582912 | tf_op jit(solution)/shard_map/apply_pairs/pallas_call | solution.py:194
  29.3 0.0 copy-start.1
  29.3 0.1 collective-permute-start
  29.4 0.0 copy-done
  29.4 4.0 %rotate_left.1 = (bf16[64,64,128]{2,1,0:T(8,128)(2,1)S(1)}, bf16[64,64,128]{2,1,0:T(8,128)(2,1)}) custom-call(s32[1]{0:T(128)} %bitcast.side_ref, bf16[64,256,128]{2,1,0:T(8,128)(2,1)} %left_ref.3, bf16[256,128]{1,0:T(8,128)(2,1)S(1)} %copy-done), custom_call_target="tpu_custom_call" | custom-call | flops 536870912 | bytes 6291456 | tf_op jit(solution)/shard_map/rotate_left/pallas_call | solution.py:48
  33.5 0.6 collective-permute-start.4
  34.0 0.0 collective-permute-done
  34.1 1.8 %collective-permute-start.1 = (bf16[2,16,768]{2,1,0:T(8,128)(2,1)S(1)}, bf16[2,16,768]{2,1,0:T(8,128)(2,1)S(1)}, u32[]{:S(2)}, u32[]{:S(2)}) collective-permute-start(bf16[2,16,768]{2,1,0:T(8,128)(2,1)S(1)} %get-tuple-element.10), channel_id=1, source_target_pairs={{0,2},{2,4},{4,6},{6,0},{1,3},{3,5},{5,7},{7,1},{8,10},{10,12},{12... | collective-permute-start | bytes 147464 | tf_op jit(solution)/shard_map/ppermute | solution.py:244
  35.9 2.6 %collective-permute-start.3 = (bf16[2,16,768]{2,1,0:T(8,128)(2,1)S(1)}, bf16[2,16,768]{2,1,0:T(8,128)(2,1)S(1)}, u32[]{:S(2)}, u32[]{:S(2)}) collective-permute-start(bf16[2,16,768]{2,1,0:T(8,128)(2,1)S(1)} %get-tuple-element.11), channel_id=1, source_target_pairs={{0,6},{2,0},{4,2},{6,4},{1,7},{3,1},{5,3},{7,5},{8,14},{10,8},{12,... | collective-permute-start | bytes 147464 | tf_op jit(solution)/shard_map/ppermute | solution.py:244
  38.4 1.4 %collective-permute-start.2 = (bf16[2,16,768]{2,1,0:T(8,128)(2,1)S(1)}, bf16[2,16,768]{2,1,0:T(8,128)(2,1)S(1)}, u32[]{:S(2)}, u32[]{:S(2)}) collective-permute-start(bf16[2,16,768]{2,1,0:T(8,128)(2,1)S(1)} %get-tuple-element.12), channel_id=1, source_target_pairs={{0,4},{2,6},{4,0},{6,2},{1,5},{3,7},{5,1},{7,3},{8,12},{10,14},{12... | collective-permute-start | bytes 147464 | tf_op jit(solution)/shard_map/ppermute | solution.py:244
  39.8 0.0 copy-done.1
  39.8 0.2 convert_reduce_fusion.1
  40.0 0.4 collective-permute-done.1
  40.4 0.0 collective-permute-done.3
  40.4 3.6 %collective-permute-done.2 = bf16[2,16,768]{2,1,0:T(8,128)(2,1)S(1)} collective-permute-done((bf16[2,16,768]{2,1,0:T(8,128)(2,1)S(1)}, bf16[2,16,768]{2,1,0:T(8,128)(2,1)S(1)}, u32[]{:S(2)}, u32[]{:S(2)}) %collective-permute-start.2) | collective-permute-done | bytes 49184 | tf_op jit(solution)/shard_map/ppermute | solution.py:244
  44.1 0.7 copy.16
  44.7 6.1 %all-to-all-start.1 = ((bf16[16,2,768]{2,1,0:T(2,128)(2,1)}), bf16[16,2,768]{2,1,0:T(2,128)(2,1)S(1)}, u32[]{:S(2)}, u32[]{:S(2)}) async-start(bf16[16,2,768]{2,1,0:T(2,128)(2,1)} %copy.16), calls=%async_computation.1 | async-start | bytes 98304 | tf_op jit(solution)/shard_map/all_to_all | solution.py:282
  50.8 0.0 collective-permute-done.4.other_ref
  50.9 2.8 %renew.1 = bf16[128,64,128]{2,1,0:T(8,128)(2,1)} custom-call(s32[1]{0:T(128)} %bitcast.side_ref, s32[1]{0:T(128)S(6)} %copy.20.count_ref, s32[64]{0:T(128)S(1)} %multiply_add_fusion.place_ref, bf16[64,64,128]{2,1,0:T(8,128)(2,1)S(1)} %get-tuple-element.8.keep_ref, bf16[64,64,128]{2,1,0:T(8,128)(2,1)S(1)} %collective-permute-done.4.other_ref, ...), custom_call_target="tpu_custom_call" | custom-call | flops 268435456 | bytes 4194304 | tf_op jit(solution)/shard_map/renew/pallas_call | solution.py:99
  53.7 4.8 %all-to-all-done.1 = bf16[16,2,768]{2,1,0:T(2,128)(2,1)S(1)} async-done(((bf16[16,2,768]{2,1,0:T(2,128)(2,1)}), bf16[16,2,768]{2,1,0:T(2,128)(2,1)S(1)}, u32[]{:S(2)}, u32[]{:S(2)}) %all-to-all-start.1) | async-done | bytes 49184 | tf_op jit(solution)/shard_map/all_to_all | solution.py:282
  58.4 4.7 %all-to-all-start.2 = ((bf16[128,64,128]{2,1,0:T(8,128)(2,1)}), bf16[128,64,128]{2,1,0:T(8,128)(2,1)S(1)}, u32[]{:S(2)}, u32[]{:S(2)}) async-start(bf16[128,64,128]{2,1,0:T(8,128)(2,1)} %renew.1), calls=%async_computation.2 | async-start | bytes 4194304 | tf_op jit(solution)/shard_map/all_to_all | solution.py:277
  63.1 0.6 convert_reduce_fusion
  63.8 26.3 %all-to-all-done.2.in_ref = bf16[128,64,128]{2,1,0:T(8,128)(2,1)S(1)} async-done(((bf16[128,64,128]{2,1,0:T(8,128)(2,1)}), bf16[128,64,128]{2,1,0:T(8,128)(2,1)S(1)}, u32[]{:S(2)}, u32[]{:S(2)}) %all-to-all-start.2) | async-done | bytes 2097184 | tf_op jit(solution)/shard_map/all_to_all | solution.py:277
  90.1 1.3 %store.1 = bf16[128,64,128]{2,1,0:T(8,128)(2,1)} custom-call(bf16[128,64,128]{2,1,0:T(8,128)(2,1)S(1)} %all-to-all-done.2.in_ref), custom_call_target="tpu_custom_call" | custom-call | flops 4194304 | bytes 4194304 | tf_op jit(solution)/shard_map/store/pallas_call | solution.py:225
  (5 shorter events, 0.1 us)
Async XLA Ops:
  2.0 21.8 %all-to-all-start = ((bf16[64,3,4,128]{3,2,1,0:T(4,128)(2,1)}), bf16[64,3,4,128]{3,2,1,0:T(4,128)(2,1)S(1)}, u32[]{:S(2)}, u32[]{:S(2)}) async-start(bf16[64,3,4,128]{3,2,1,0:T(4,128)(2,1)} %broadcast_in_dim.8), calls=%async_computation | async-start | bytes 393216 | tf_op jit(solution)/shard_map/all_to_all | solution.py:255
  24.1 5.3 %copy-start = (bf16[256,128]{1,0:T(8,128)(2,1)S(1)}, bf16[256,128]{1,0:T(8,128)(2,1)}, u32[]{:S(2)}) copy-start(bf16[256,128]{1,0:T(8,128)(2,1)} %rot_ref.3) | copy-start | bytes 196612
  29.3 10.5 %copy-start.1 = (s32[64,1]{0,1:T(1,128)S(1)}, s32[64,1]{0,1:T(1,128)}, u32[]{:S(2)}) copy-start(s32[64,1]{0,1:T(1,128)} %param.11) | copy-start | bytes 772
  29.3 4.7 %collective-permute-start = (bf16[4,2,16,768]{3,2,1,0:T(8,128)(2,1)S(1)}, bf16[4,2,16,768]{3,2,1,0:T(8,128)(2,1)S(1)}, u32[]{:S(2)}, u32[]{:S(2)}) collective-permute-start(bf16[4,2,16,768]{3,2,1,0:T(8,128)(2,1)S(1)} %get-tuple-element.7), channel_id=1, source_target_pairs={{0,1},{1,0},{2,3},{3,2},{4,5},{5,4},{6,7},{7,6},{8,9},{9,8},{10,11... | collective-permute-start | bytes 589832 | tf_op jit(solution)/shard_map/ppermute | solution.py:279
  33.5 17.4 %collective-permute-start.4 = (bf16[64,64,128]{2,1,0:T(8,128)(2,1)}, bf16[64,64,128]{2,1,0:T(8,128)(2,1)S(1)}, u32[]{:S(2)}, u32[]{:S(2)}) collective-permute-start(bf16[64,64,128]{2,1,0:T(8,128)(2,1)} %get-tuple-element.9), channel_id=1, source_target_pairs={{0,1},{1,0},{2,3},{3,2},{4,5},{5,4},{6,7},{7,6},{8,9},{9,8},{10,11... | collective-permute-start | bytes 3145736 | tf_op jit(solution)/shard_map/ppermute | solution.py:274
  34.1 6.3 %collective-permute-start.1 = (bf16[2,16,768]{2,1,0:T(8,128)(2,1)S(1)}, bf16[2,16,768]{2,1,0:T(8,128)(2,1)S(1)}, u32[]{:S(2)}, u32[]{:S(2)}) collective-permute-start(bf16[2,16,768]{2,1,0:T(8,128)(2,1)S(1)} %get-tuple-element.10), channel_id=1, source_target_pairs={{0,2},{2,4},{4,6},{6,0},{1,3},{3,5},{5,7},{7,1},{8,10},{10,12},{12... | collective-permute-start | bytes 147464 | tf_op jit(solution)/shard_map/ppermute | solution.py:244
  35.9 4.6 %collective-permute-start.3 = (bf16[2,16,768]{2,1,0:T(8,128)(2,1)S(1)}, bf16[2,16,768]{2,1,0:T(8,128)(2,1)S(1)}, u32[]{:S(2)}, u32[]{:S(2)}) collective-permute-start(bf16[2,16,768]{2,1,0:T(8,128)(2,1)S(1)} %get-tuple-element.11), channel_id=1, source_target_pairs={{0,6},{2,0},{4,2},{6,4},{1,7},{3,1},{5,3},{7,5},{8,14},{10,8},{12,... | collective-permute-start | bytes 147464 | tf_op jit(solution)/shard_map/ppermute | solution.py:244
  38.4 5.6 %collective-permute-start.2 = (bf16[2,16,768]{2,1,0:T(8,128)(2,1)S(1)}, bf16[2,16,768]{2,1,0:T(8,128)(2,1)S(1)}, u32[]{:S(2)}, u32[]{:S(2)}) collective-permute-start(bf16[2,16,768]{2,1,0:T(8,128)(2,1)S(1)} %get-tuple-element.12), channel_id=1, source_target_pairs={{0,4},{2,6},{4,0},{6,2},{1,5},{3,7},{5,1},{7,3},{8,12},{10,14},{12... | collective-permute-start | bytes 147464 | tf_op jit(solution)/shard_map/ppermute | solution.py:244
  44.7 13.7 %all-to-all-start.1 = ((bf16[16,2,768]{2,1,0:T(2,128)(2,1)}), bf16[16,2,768]{2,1,0:T(2,128)(2,1)S(1)}, u32[]{:S(2)}, u32[]{:S(2)}) async-start(bf16[16,2,768]{2,1,0:T(2,128)(2,1)} %copy.16), calls=%async_computation.1 | async-start | bytes 98304 | tf_op jit(solution)/shard_map/all_to_all | solution.py:282
  58.4 31.7 %all-to-all-start.2 = ((bf16[128,64,128]{2,1,0:T(8,128)(2,1)}), bf16[128,64,128]{2,1,0:T(8,128)(2,1)S(1)}, u32[]{:S(2)}, u32[]{:S(2)}) async-start(bf16[128,64,128]{2,1,0:T(8,128)(2,1)} %renew.1), calls=%async_computation.2 | async-start | bytes 4194304 | tf_op jit(solution)/shard_map/all_to_all | solution.py:277

commit v2 on v1

--- a/solution.py
+++ b/solution.py
@@ -7,8 +7,10 @@
 from jax.sharding import PartitionSpec as P
 
 
-OPS = ("ops_0", "ops_1", "ops_2")
-ALL = ("ops_0", "ops_1", "ops_2", "blk")
+OPS = ("y", "x_hi", "x_lo", "z")
+FIRST = ("x_hi", "z")
+LAST = ("x_lo", "y")
+ALL = OPS + ("blk",)
 GROUP = 8
 MIB = 1 << 20
 LANES = 128
@@ -168,25 +170,35 @@
         return carry
 
     lax.fori_loop(0, groups, step, 0)
-    ring = keep_ref.shape[0]
-    span = rows // keep_ref.shape[2]
     side = side_ref[0]
-    for z in range(ring):
+    outer = keep_ref.shape[2] // 2
+    span = rows // outer
+    ring = keep_ref.shape[0] // 2
+    unit = span // (4 * ring)
+    for group in range(2 * ring):
         for u in range(2):
-            at = z * (span // ring) + u
+            at = (group // ring * 2 * ring + group % ring) * unit + u
             for c in range(total.shape[0]):
                 lanes = slice(c * LANES, (c + 1) * LANES)
-                mine = total[c, pl.ds(at + 2 * side, keep_ref.shape[2], stride=span)]
-                theirs = total[c, pl.ds(at + 2 - 2 * side, keep_ref.shape[2], stride=span)]
-                keep_ref[z, u, :, lanes] = mine
-                send_ref[z, u, :, lanes] = theirs.astype(send_ref.dtype)
-
-
-def apply_pairs(side, count, wave, operators_left, operators_right):
+
+                def lines(half):
+                    return jnp.concatenate(
+                        [
+                            total[c, pl.ds(at + low * ring * unit + 2 * half, outer, stride=span)]
+                            for low in range(2)
+                        ],
+                        axis=0,
+                    )
+
+                keep_ref[group, u, :, lanes] = lines(side)
+                send_ref[group, u, :, lanes] = lines(1 - side).astype(send_ref.dtype)
+
+
+def apply_pairs(near, side, count, wave, operators_left, operators_right):
     slots, rows, cols = operators_left.shape
     right = operators_right.shape[1]
     vectors = wave.shape[0] // cols
-    part = (4, 2, rows // 16, vectors * right)
+    part = (near, 2, rows // (4 * near), vectors * right)
     smem = pl.BlockSpec(memory_space=pltpu.SMEM)
     vmem = pl.BlockSpec(memory_space=pltpu.VMEM)
     hbm = pl.BlockSpec(memory_space=pltpu.HBM)
@@ -234,15 +246,21 @@
     )(x)
 
 
-def own_share(blocks, axis):
-    size = lax.axis_size(axis)
-    me = lax.axis_index(axis)
+def own_share(blocks, axes):
+    first, second = (lax.axis_size(axis) for axis in axes)
+    here = [lax.axis_index(axis) for axis in axes]
+    own = here[0] * second + here[1]
     parts = []
-    for k in range(1, size):
-        block = lax.dynamic_index_in_dim(blocks, (me + k) % size, 0, keepdims=False)
-        hop = [(i, (i + k) % size) for i in range(size)]
-        parts.append(lax.ppermute(block.astype(jnp.bfloat16), axis, hop))
-    total = lax.dynamic_index_in_dim(blocks, me, 0, keepdims=False)
+    for k in range(1, first * second):
+        far, near = k // second, k % second
+
+        def target(i, j):
+            return (i + far) % first * second + (j + near) % second
+
+        hop = [(i * second + j, target(i, j)) for i in range(first) for j in range(second)]
+        block = lax.dynamic_index_in_dim(blocks, target(*here), 0, keepdims=False)
+        parts.append(lax.ppermute(block.astype(jnp.bfloat16), axes, hop))
+    total = lax.dynamic_index_in_dim(blocks, own, 0, keepdims=False)
     for part in parts:
         total = total + part.astype(jnp.float32)
     return total
@@ -275,11 +293,11 @@
     wave = gather_wave(wavefunction)
     outgoing = renew(side, pair_count, places, keep, other, rotation, owners * capacity)
     incoming = lax.all_to_all(outgoing, OPS, split_axis=0, concat_axis=0, tiled=True)
-    mine, theirs = apply_pairs(side, pair_count, wave, operators_left, operators_right)
+    mine, theirs = apply_pairs(lax.axis_size(FIRST), side, pair_count, wave, operators_left, operators_right)
     got = lax.ppermute(theirs, "blk", [(0, 1), (1, 0)])
-    mine = own_share(mine + got.astype(jnp.float32), "ops_2")
+    mine = own_share(mine + got.astype(jnp.float32), FIRST)
     parts = jnp.transpose(mine.astype(jnp.bfloat16), (1, 0, 2))
-    parts = lax.all_to_all(parts, ("ops_0", "ops_1"), 0, 0, tiled=True)
+    parts = lax.all_to_all(parts, LAST, 0, 0, tiled=True)
     renewed = store(incoming)
     sigma = jnp.sum(parts.astype(jnp.float32), axis=0)
     sigma = sigma.reshape(left_states // (2 * owners), vectors, right_states)
@@ -287,7 +305,7 @@
 
 
 def solution(mesh):
-    split = Mesh(mesh.devices.reshape(4, 4, 4, mesh.shape["blk"]), ALL)
+    split = Mesh(mesh.devices.reshape(4, 2, 2, 4, mesh.shape["blk"]), ALL)
     placed = (
         P(OPS, None, "blk"),
         P(OPS, None, None),

time: 91.8 us -> 99.1 us (1.080)
  starting transfers between devices: 28.7 us -> 35.6 us
    ppermute x3 -> x7, starting transfers between devices: 5.73 us -> 13.8 us  [own_share(): parts.append(lax.ppermute(block.astype(jnp.bfloat16), axes, hop))]
    all_to_all x1, starting transfers between devices: 6.1 us -> 3.33 us  [per_device(): parts = lax.all_to_all(parts, LAST, 0, 0, tiled=True)]
    ppermute x3 -> x7, waiting for transfers between devices: 4.03 us -> 6.25 us  [own_share(): parts.append(lax.ppermute(block.astype(jnp.bfloat16), axes, hop))]
    all_to_all x1, starting transfers between devices: 4.69 us -> 6.24 us  [per_device(): lax.all_to_all(outgoing, OPS, split_axis=0, concat_axis=0, tiled=True)]
    all_to_all x1, waiting for transfers between devices: 4.77 us -> 3.34 us  [per_device(): parts = lax.all_to_all(parts, LAST, 0, 0, tiled=True)]
  transfers between devices with their start and end apart: 8 -> 12, of which waited for: 5 -> 7; matrix products, arithmetic and copies ran while one was open for 2% -> 2% of each run, Pallas kernels for 7% -> 7%
where the time goes in v2:
time: 99.1 us; the launch traced here: 98.7 us
  waiting for transfers between devices  44.8 us (45%)
  starting transfers between devices  35.6 us (36%)
  Pallas kernels  13.6 us (14%)
  local copies, waits for them, and re-layouts  2.38 us (2%)
  between operations  1.41 us (1%)
    all_to_all x1, waiting for transfers between devices, per_device(): lax.all_to_all(outgoing, OPS, split_axis=0, concat_axis=0, tiled=True)  25.6 us
    ppermute x7, starting transfers between devices, own_share(): parts.append(lax.ppermute(block.astype(jnp.bfloat16), axes, hop))  13.8 us
    all_to_all x1, starting transfers between devices, gather_wave(): lax.all_to_all(jnp.broadcast_to(shard, (owners, *shard.shape)), OPS, 0, 0...  11.5 us
    all_to_all x1, waiting for transfers between devices, gather_wave(): lax.all_to_all(jnp.broadcast_to(shard, (owners, *shard.shape)), OPS, 0, 0...  9.58 us
    ppermute x7, waiting for transfers between devices, own_share(): parts.append(lax.ppermute(block.astype(jnp.bfloat16), axes, hop))  6.25 us
    all_to_all x1, starting transfers between devices, per_device(): lax.all_to_all(outgoing, OPS, split_axis=0, concat_axis=0, tiled=True)  6.24 us
    pallas_call x1, Pallas kernels, apply_pairs(): pl.pallas_call(sigma_kernel, in_specs=[smem, smem, vmem, hbm, hbm], out_s...  5.42 us
    pallas_call x1, Pallas kernels, rotate_left(): pl.pallas_call(rotate_kernel, in_specs=[pl.BlockSpec(memory_space=pltpu.S...  4.04 us
  transfers between devices with their start and end apart: 12, of which 7 were waited for; matrix products, arithmetic and copies ran while one was open for 2% of the time, Pallas kernels for 7%

profile of v2, /device:TPU:0, one launch (start us, length us, event | category | flops | bytes accessed | tf_op | source)
XLA Modules:
  0.0 98.7 jit_solution(11840675827141225944)
XLA Ops:
  0.6 1.4 %broadcast_in_dim.8 = bf16[64,3,4,128]{3,2,1,0:T(4,128)(2,1)} broadcast(bf16[3,4,128]{2,1,0:T(4,128)(2,1)} %bitcast.53), dimensions={1,2,3} | broadcast | bytes 199680 | tf_op jit(solution)/shard_map/broadcast_in_dim | solution.py:274
  2.0 11.5 %all-to-all-start = ((bf16[64,3,4,128]{3,2,1,0:T(4,128)(2,1)}), bf16[64,3,4,128]{3,2,1,0:T(4,128)(2,1)S(1)}, u32[]{:S(2)}, u32[]{:S(2)}) async-start(bf16[64,3,4,128]{3,2,1,0:T(4,128)(2,1)} %broadcast_in_dim.8), calls=%async_computation | async-start | bytes 393216 | tf_op jit(solution)/shard_map/all_to_all | solution.py:273
  14.2 9.6 %all-to-all-done = bf16[64,3,4,128]{3,2,1,0:T(4,128)(2,1)S(1)} async-done(((bf16[64,3,4,128]{3,2,1,0:T(4,128)(2,1)}), bf16[64,3,4,128]{3,2,1,0:T(4,128)(2,1)S(1)}, u32[]{:S(2)}, u32[]{:S(2)}) %all-to-all-start) | async-done | bytes 196640 | tf_op jit(solution)/shard_map/all_to_all | solution.py:273
  23.8 0.1 copy.14
  24.0 0.1 copy.15.wave_ref
  24.1 0.0 copy-start
  24.1 5.4 %apply_pairs.1 = (f32[8,2,8,768]{3,2,1,0:T(8,128)S(1)}, bf16[8,2,8,768]{3,2,1,0:T(8,128)(2,1)S(1)}) custom-call(s32[1]{0:T(128)} %bitcast.side_ref, s32[1]{0:T(128)S(6)} %copy.20.count_ref, bf16[384,256]{1,0:T(8,128)(2,1)S(1)} %copy.15.wave_ref, bf16[64,256,128]{2,1,0:T(8,128)(2,1)} %left_ref.3, bf16[64,256,256]{2,1,0:T(8,128)(2,1)} %right_ref.1), custom_call_target="tpu_custom_call" | custom-call | flops 6442450944 | bytes 12582912 | tf_op jit(solution)/shard_map/apply_pairs/pallas_call | solution.py:206
  29.5 0.0 copy-start.1
  29.6 0.1 collective-permute-start
  29.6 0.0 copy-done
  29.7 4.0 %rotate_left.1 = (bf16[64,64,128]{2,1,0:T(8,128)(2,1)S(1)}, bf16[64,64,128]{2,1,0:T(8,128)(2,1)}) custom-call(s32[1]{0:T(128)} %bitcast.side_ref, bf16[64,256,128]{2,1,0:T(8,128)(2,1)} %left_ref.3, bf16[256,128]{1,0:T(8,128)(2,1)S(1)} %copy-done), custom_call_target="tpu_custom_call" | custom-call | flops 536870912 | bytes 6291456 | tf_op jit(solution)/shard_map/rotate_left/pallas_call | solution.py:50
  33.7 0.6 collective-permute-start.8
  34.3 0.0 collective-permute-done
  34.4 1.8 %collective-permute-start.1 = (bf16[2,8,768]{2,1,0:T(8,128)(2,1)S(1)}, bf16[2,8,768]{2,1,0:T(8,128)(2,1)S(1)}, u32[]{:S(2)}, u32[]{:S(2)}) collective-permute-start(bf16[2,8,768]{2,1,0:T(8,128)(2,1)S(1)} %get-tuple-element.10), channel_id=1, source_target_pairs={{0,2},{2,4},{4,6},{6,0},{16,18},{18,20},{20,22},{22,16},{1,3},{3,5... | collective-permute-start | bytes 73736 | tf_op jit(solution)/shard_map/ppermute | solution.py:262
  36.1 5.2 %collective-permute-start.7 = (bf16[2,8,768]{2,1,0:T(8,128)(2,1)S(1)}, bf16[2,8,768]{2,1,0:T(8,128)(2,1)S(1)}, u32[]{:S(2)}, u32[]{:S(2)}) collective-permute-start(bf16[2,8,768]{2,1,0:T(8,128)(2,1)S(1)} %get-tuple-element.11), channel_id=1, source_target_pairs={{0,22},{2,16},{4,18},{6,20},{16,6},{18,0},{20,2},{22,4},{1,23},{3,... | collective-permute-start | bytes 73736 | tf_op jit(solution)/shard_map/ppermute | solution.py:262
  41.4 0.0 collective-permute-start.6
  41.4 0.0 copy-done.1
  41.4 0.2 convert_reduce_fusion.1
  41.5 3.6 %collective-permute-start.5 = (bf16[2,8,768]{2,1,0:T(8,128)(2,1)S(1)}, bf16[2,8,768]{2,1,0:T(8,128)(2,1)S(1)}, u32[]{:S(2)}, u32[]{:S(2)}) collective-permute-start(bf16[2,8,768]{2,1,0:T(8,128)(2,1)S(1)} %get-tuple-element.13), channel_id=1, source_target_pairs={{0,18},{2,20},{4,22},{6,16},{16,2},{18,4},{20,6},{22,0},{1,19},{3,... | collective-permute-start | bytes 73736 | tf_op jit(solution)/shard_map/ppermute | solution.py:262
  45.1 0.0 collective-permute-done.1
  45.1 2.0 %collective-permute-start.4 = (bf16[2,8,768]{2,1,0:T(8,128)(2,1)S(1)}, bf16[2,8,768]{2,1,0:T(8,128)(2,1)S(1)}, u32[]{:S(2)}, u32[]{:S(2)}) collective-permute-start(bf16[2,8,768]{2,1,0:T(8,128)(2,1)S(1)} %get-tuple-element.14), channel_id=1, source_target_pairs={{0,16},{2,18},{4,20},{6,22},{16,0},{18,2},{20,4},{22,6},{1,17},{3,... | collective-permute-start | bytes 73736 | tf_op jit(solution)/shard_map/ppermute | solution.py:262
  47.1 0.0 collective-permute-done.7
  47.1 0.7 collective-permute-start.3
  47.8 1.5 %collective-permute-done.6 = bf16[2,8,768]{2,1,0:T(8,128)(2,1)S(1)} collective-permute-done((bf16[2,8,768]{2,1,0:T(8,128)(2,1)S(1)}, bf16[2,8,768]{2,1,0:T(8,128)(2,1)S(1)}, u32[]{:S(2)}, u32[]{:S(2)}) %collective-permute-start.6) | collective-permute-done | bytes 24608 | tf_op jit(solution)/shard_map/ppermute | solution.py:262
  49.3 0.6 collective-permute-start.2
  49.9 0.0 collective-permute-done.5
  49.9 0.6 collective-permute-done.4
  50.5 0.5 collective-permute-done.3
  51.0 3.7 %collective-permute-done.2 = bf16[2,8,768]{2,1,0:T(8,128)(2,1)S(1)} collective-permute-done((bf16[2,8,768]{2,1,0:T(8,128)(2,1)S(1)}, bf16[2,8,768]{2,1,0:T(8,128)(2,1)S(1)}, u32[]{:S(2)}, u32[]{:S(2)}) %collective-permute-start.2) | collective-permute-done | bytes 24608 | tf_op jit(solution)/shard_map/ppermute | solution.py:262
  54.7 0.6 copy.16
  55.3 3.3 %all-to-all-start.1 = ((bf16[8,2,768]{2,1,0:T(2,128)(2,1)}), bf16[8,2,768]{2,1,0:T(2,128)(2,1)S(1)}, u32[]{:S(2)}, u32[]{:S(2)}) async-start(bf16[8,2,768]{2,1,0:T(2,128)(2,1)} %copy.16), calls=%async_computation.1 | async-start | bytes 49152 | tf_op jit(solution)/shard_map/all_to_all | solution.py:300
  58.7 0.0 collective-permute-done.8.other_ref
  58.7 2.8 %renew.1 = bf16[128,64,128]{2,1,0:T(8,128)(2,1)} custom-call(s32[1]{0:T(128)} %bitcast.side_ref, s32[1]{0:T(128)S(6)} %copy.20.count_ref, s32[64]{0:T(128)S(1)} %multiply_add_fusion.place_ref, bf16[64,64,128]{2,1,0:T(8,128)(2,1)S(1)} %get-tuple-element.8.keep_ref, bf16[64,64,128]{2,1,0:T(8,128)(2,1)S(1)} %collective-permute-done.8.other_ref, ...), custom_call_target="tpu_custom_call" | custom-call | flops 268435456 | bytes 4194304 | tf_op jit(solution)/shard_map/renew/pallas_call | solution.py:101
  61.5 3.3 %all-to-all-done.1 = bf16[8,2,768]{2,1,0:T(2,128)(2,1)S(1)} async-done(((bf16[8,2,768]{2,1,0:T(2,128)(2,1)}), bf16[8,2,768]{2,1,0:T(2,128)(2,1)S(1)}, u32[]{:S(2)}, u32[]{:S(2)}) %all-to-all-start.1) | async-done | bytes 24608 | tf_op jit(solution)/shard_map/all_to_all | solution.py:300
  64.8 6.2 %all-to-all-start.2 = ((bf16[128,64,128]{2,1,0:T(8,128)(2,1)}), bf16[128,64,128]{2,1,0:T(8,128)(2,1)S(1)}, u32[]{:S(2)}, u32[]{:S(2)}) async-start(bf16[128,64,128]{2,1,0:T(8,128)(2,1)} %renew.1), calls=%async_computation.2 | async-start | bytes 4194304 | tf_op jit(solution)/shard_map/all_to_all | solution.py:295
  71.1 0.6 convert_reduce_fusion
  71.7 25.6 %all-to-all-done.2.in_ref = bf16[128,64,128]{2,1,0:T(8,128)(2,1)S(1)} async-done(((bf16[128,64,128]{2,1,0:T(8,128)(2,1)}), bf16[128,64,128]{2,1,0:T(8,128)(2,1)S(1)}, u32[]{:S(2)}, u32[]{:S(2)}) %all-to-all-start.2) | async-done | bytes 2097184 | tf_op jit(solution)/shard_map/all_to_all | solution.py:295
  97.3 1.3 %store.1 = bf16[128,64,128]{2,1,0:T(8,128)(2,1)} custom-call(bf16[128,64,128]{2,1,0:T(8,128)(2,1)S(1)} %all-to-all-done.2.in_ref), custom_call_target="tpu_custom_call" | custom-call | flops 4194304 | bytes 4194304 | tf_op jit(solution)/shard_map/store/pallas_call | solution.py:237
  (5 shorter events, 0.1 us)
Async XLA Ops:
  2.0 21.8 %all-to-all-start = ((bf16[64,3,4,128]{3,2,1,0:T(4,128)(2,1)}), bf16[64,3,4,128]{3,2,1,0:T(4,128)(2,1)S(1)}, u32[]{:S(2)}, u32[]{:S(2)}) async-start(bf16[64,3,4,128]{3,2,1,0:T(4,128)(2,1)} %broadcast_in_dim.8), calls=%async_computation | async-start | bytes 393216 | tf_op jit(solution)/shard_map/all_to_all | solution.py:273
  24.1 5.5 %copy-start = (bf16[256,128]{1,0:T(8,128)(2,1)S(1)}, bf16[256,128]{1,0:T(8,128)(2,1)}, u32[]{:S(2)}) copy-start(bf16[256,128]{1,0:T(8,128)(2,1)} %rot_ref.3) | copy-start | bytes 196612
  29.5 11.8 %copy-start.1 = (s32[64,1]{0,1:T(1,128)S(1)}, s32[64,1]{0,1:T(1,128)}, u32[]{:S(2)}) copy-start(s32[64,1]{0,1:T(1,128)} %param.11) | copy-start | bytes 772
  29.6 4.7 %collective-permute-start = (bf16[8,2,8,768]{3,2,1,0:T(8,128)(2,1)S(1)}, bf16[8,2,8,768]{3,2,1,0:T(8,128)(2,1)S(1)}, u32[]{:S(2)}, u32[]{:S(2)}) collective-permute-start(bf16[8,2,8,768]{3,2,1,0:T(8,128)(2,1)S(1)} %get-tuple-element.7), channel_id=1, source_target_pairs={{0,1},{1,0},{2,3},{3,2},{4,5},{5,4},{6,7},{7,6},{8,9},{9,8},{10,11... | collective-permute-start | bytes 589832 | tf_op jit(solution)/shard_map/ppermute | solution.py:297
  33.7 24.9 %collective-permute-start.8 = (bf16[64,64,128]{2,1,0:T(8,128)(2,1)}, bf16[64,64,128]{2,1,0:T(8,128)(2,1)S(1)}, u32[]{:S(2)}, u32[]{:S(2)}) collective-permute-start(bf16[64,64,128]{2,1,0:T(8,128)(2,1)} %get-tuple-element.9), channel_id=1, source_target_pairs={{0,1},{1,0},{2,3},{3,2},{4,5},{5,4},{6,7},{7,6},{8,9},{9,8},{10,11... | collective-permute-start | bytes 3145736 | tf_op jit(solution)/shard_map/ppermute | solution.py:292
  34.4 10.8 %collective-permute-start.1 = (bf16[2,8,768]{2,1,0:T(8,128)(2,1)S(1)}, bf16[2,8,768]{2,1,0:T(8,128)(2,1)S(1)}, u32[]{:S(2)}, u32[]{:S(2)}) collective-permute-start(bf16[2,8,768]{2,1,0:T(8,128)(2,1)S(1)} %get-tuple-element.10), channel_id=1, source_target_pairs={{0,2},{2,4},{4,6},{6,0},{16,18},{18,20},{20,22},{22,16},{1,3},{3,5... | collective-permute-start | bytes 73736 | tf_op jit(solution)/shard_map/ppermute | solution.py:262
  36.1 11.0 %collective-permute-start.7 = (bf16[2,8,768]{2,1,0:T(8,128)(2,1)S(1)}, bf16[2,8,768]{2,1,0:T(8,128)(2,1)S(1)}, u32[]{:S(2)}, u32[]{:S(2)}) collective-permute-start(bf16[2,8,768]{2,1,0:T(8,128)(2,1)S(1)} %get-tuple-element.11), channel_id=1, source_target_pairs={{0,22},{2,16},{4,18},{6,20},{16,6},{18,0},{20,2},{22,4},{1,23},{3,... | collective-permute-start | bytes 73736 | tf_op jit(solution)/shard_map/ppermute | solution.py:262
  41.4 8.0 %collective-permute-start.6 = (bf16[2,8,768]{2,1,0:T(8,128)(2,1)S(1)}, bf16[2,8,768]{2,1,0:T(8,128)(2,1)S(1)}, u32[]{:S(2)}, u32[]{:S(2)}) collective-permute-start(bf16[2,8,768]{2,1,0:T(8,128)(2,1)S(1)} %get-tuple-element.12), channel_id=1, source_target_pairs={{0,20},{2,22},{4,16},{6,18},{16,4},{18,6},{20,0},{22,2},{1,21},{3,... | collective-permute-start | bytes 73736 | tf_op jit(solution)/shard_map/ppermute | solution.py:262
  41.5 8.3 %collective-permute-start.5 = (bf16[2,8,768]{2,1,0:T(8,128)(2,1)S(1)}, bf16[2,8,768]{2,1,0:T(8,128)(2,1)S(1)}, u32[]{:S(2)}, u32[]{:S(2)}) collective-permute-start(bf16[2,8,768]{2,1,0:T(8,128)(2,1)S(1)} %get-tuple-element.13), channel_id=1, source_target_pairs={{0,18},{2,20},{4,22},{6,16},{16,2},{18,4},{20,6},{22,0},{1,19},{3,... | collective-permute-start | bytes 73736 | tf_op jit(solution)/shard_map/ppermute | solution.py:262
  45.1 5.3 %collective-permute-start.4 = (bf16[2,8,768]{2,1,0:T(8,128)(2,1)S(1)}, bf16[2,8,768]{2,1,0:T(8,128)(2,1)S(1)}, u32[]{:S(2)}, u32[]{:S(2)}) collective-permute-start(bf16[2,8,768]{2,1,0:T(8,128)(2,1)S(1)} %get-tuple-element.14), channel_id=1, source_target_pairs={{0,16},{2,18},{4,20},{6,22},{16,0},{18,2},{20,4},{22,6},{1,17},{3,... | collective-permute-start | bytes 73736 | tf_op jit(solution)/shard_map/ppermute | solution.py:262
  47.1 3.8 %collective-permute-start.3 = (bf16[2,8,768]{2,1,0:T(8,128)(2,1)S(1)}, bf16[2,8,768]{2,1,0:T(8,128)(2,1)S(1)}, u32[]{:S(2)}, u32[]{:S(2)}) collective-permute-start(bf16[2,8,768]{2,1,0:T(8,128)(2,1)S(1)} %get-tuple-element.15), channel_id=1, source_target_pairs={{0,6},{2,0},{4,2},{6,4},{16,22},{18,16},{20,18},{22,20},{1,7},{3,1... | collective-permute-start | bytes 73736 | tf_op jit(solution)/shard_map/ppermute | solution.py:262
  49.3 5.3 %collective-permute-start.2 = (bf16[2,8,768]{2,1,0:T(8,128)(2,1)S(1)}, bf16[2,8,768]{2,1,0:T(8,128)(2,1)S(1)}, u32[]{:S(2)}, u32[]{:S(2)}) collective-permute-start(bf16[2,8,768]{2,1,0:T(8,128)(2,1)S(1)} %get-tuple-element.16), channel_id=1, source_target_pairs={{0,4},{2,6},{4,0},{6,2},{16,20},{18,22},{20,16},{22,18},{1,5},{3,7... | collective-permute-start | bytes 73736 | tf_op jit(solution)/shard_map/ppermute | solution.py:262
  55.3 9.5 %all-to-all-start.1 = ((bf16[8,2,768]{2,1,0:T(2,128)(2,1)}), bf16[8,2,768]{2,1,0:T(2,128)(2,1)S(1)}, u32[]{:S(2)}, u32[]{:S(2)}) async-start(bf16[8,2,768]{2,1,0:T(2,128)(2,1)} %copy.16), calls=%async_computation.1 | async-start | bytes 49152 | tf_op jit(solution)/shard_map/all_to_all | solution.py:300
  64.8 32.5 %all-to-all-start.2 = ((bf16[128,64,128]{2,1,0:T(8,128)(2,1)}), bf16[128,64,128]{2,1,0:T(8,128)(2,1)S(1)}, u32[]{:S(2)}, u32[]{:S(2)}) async-start(bf16[128,64,128]{2,1,0:T(8,128)(2,1)} %renew.1), calls=%async_computation.2 | async-start | bytes 4194304 | tf_op jit(solution)/shard_map/all_to_all | solution.py:295

commit v3 on v2

--- a/solution.py
+++ b/solution.py
@@ -1,3 +1,5 @@
+import functools
+
 import jax
 import jax.numpy as jnp
 from jax import lax
@@ -16,13 +18,14 @@
 LANES = 128
 
 
-def rotate_kernel(side_ref, left_ref, rot_ref, keep_ref, send_ref, lefts, turned, arrived):
+def rotate_kernel(start, side_ref, left_ref, rot_ref, keep_ref, send_ref, lefts, turned, arrived):
     slots, half, width = keep_ref.shape
     groups = slots // GROUP
 
     def fetch(g):
         part = pl.ds(g * GROUP, GROUP)
-        return pltpu.make_async_copy(left_ref.at[part], lefts.at[part], arrived.at[g])
+        there = pl.ds(start + g * GROUP, GROUP)
+        return pltpu.make_async_copy(left_ref.at[there], lefts.at[part], arrived.at[g])
 
     for g in range(groups):
         fetch(g).start()
@@ -42,13 +45,13 @@
                 send_ref[p + q] = send[:, q * width : (q + 1) * width]
 
 
-def rotate_left(side, operators_left, rotation):
-    slots, rows, cols = operators_left.shape
+def rotate_left(side, operators_left, rotation, start, slots):
+    _, rows, cols = operators_left.shape
     new = rotation.shape[1]
     half = jax.ShapeDtypeStruct((slots, new // 2, cols), jnp.bfloat16)
     vmem = pl.BlockSpec(memory_space=pltpu.VMEM)
     return pl.pallas_call(
-        rotate_kernel,
+        functools.partial(rotate_kernel, start),
         in_specs=[
             pl.BlockSpec(memory_space=pltpu.SMEM),
             pl.BlockSpec(memory_space=pltpu.HBM),
@@ -71,8 +74,11 @@
     )(side, operators_left, rotation)
 
 
-def renew_kernel(side_ref, count_ref, place_ref, keep_ref, other_ref, rot_ref, out_ref):
-    slots, half, width = keep_ref.shape
+def renew_kernel(side_ref, count_ref, place_ref, rot_ref, *refs):
+    *pieces, out_ref = refs
+    keeps, others = pieces[: len(pieces) // 2], pieces[len(pieces) // 2 :]
+    piece, half, width = keeps[0].shape
+    slots = piece * len(keeps)
     live = count_ref[0]
     own_low = side_ref[0] == 0
     top, bottom = rot_ref[:width], rot_ref[width:]
@@ -81,8 +87,9 @@
     rot = jnp.concatenate([rot_own, rot_far], axis=0)
     out_ref[...] = jnp.zeros_like(out_ref)
     for first in range(slots - GROUP, -1, -GROUP):
+        group = slice(first % piece, first % piece + GROUP)
         w = jnp.concatenate(
-            [keep_ref[first : first + GROUP], other_ref[first : first + GROUP]], axis=2
+            [keeps[first // piece][group], others[first // piece][group]], axis=2
         ).reshape(GROUP * half, 2 * width)
         b = jnp.dot(w, rot, preferred_element_type=jnp.float32).astype(jnp.bfloat16)
         for q in range(GROUP - 1, -1, -1):
@@ -93,14 +100,15 @@
             )
 
 
-def renew(side, count, places, keep, other, rotation, total):
-    slots, half, width = keep.shape
+def renew(side, count, places, keeps, others, rotation, total):
+    piece, half, width = keeps[0].shape
+    slots = piece * len(keeps)
     new = rotation.shape[1]
     smem = pl.BlockSpec(memory_space=pltpu.SMEM)
     vmem = pl.BlockSpec(memory_space=pltpu.VMEM)
     return pl.pallas_call(
         renew_kernel,
-        in_specs=[smem, smem, smem, vmem, vmem, vmem],
+        in_specs=[smem, smem, smem] + [vmem] * (1 + 2 * len(keeps)),
         out_specs=vmem,
         out_shape=jax.ShapeDtypeStruct((total, half, new), jnp.bfloat16),
         cost_estimate=pl.CostEstimate(
@@ -110,7 +118,7 @@
         ),
         compiler_params=pltpu.CompilerParams(vmem_limit_bytes=12 * MIB),
         name="renew",
-    )(side, count, places, keep, other, rotation)
+    )(side, count, places, rotation, *keeps, *others)
 
 
 def sigma_kernel(
@@ -288,10 +296,13 @@
     same = (targets[:, None] == targets[None, :]) & (order[None, :] < order[:, None])
     places = targets * capacity + jnp.sum(same.astype(jnp.int32), axis=1)
 
-    keep, send = rotate_left(side, operators_left, rotation)
-    other = lax.ppermute(send, "blk", [(0, 1), (1, 0)])
+    keeps, others = [], []
+    for start in range(0, slots, slots // 2):
+        keep, send = rotate_left(side, operators_left, rotation, start, slots // 2)
+        others.append(lax.ppermute(send, "blk", [(0, 1), (1, 0)]))
+        keeps.append(keep)
     wave = gather_wave(wavefunction)
-    outgoing = renew(side, pair_count, places, keep, other, rotation, owners * capacity)
+    outgoing = renew(side, pair_count, places, keeps, others, rotation, owners * capacity)
     incoming = lax.all_to_all(outgoing, OPS, split_axis=0, concat_axis=0, tiled=True)
     mine, theirs = apply_pairs(lax.axis_size(FIRST), side, pair_count, wave, operators_left, operators_right)
     got = lax.ppermute(theirs, "blk", [(0, 1), (1, 0)])

time: 99.1 us -> 102 us (1.029)
  starting transfers between devices: 35.6 us -> 37 us
    pallas_call x2 -> x3, Pallas kernels: 6.87 us -> 6.92 us  [the longest x2 4.11 us: rotate_left(): pl.pallas_call(functools.partial(rotate_kernel, start), in_specs=[pl.Bloc...]
  transfers between devices with their start and end apart: 12 -> 13, of which waited for: 7 -> 6; matrix products, arithmetic and copies ran while one was open for 2% -> 2% of each run, Pallas kernels for 7% -> 7%
where the time goes in v3:
time: 102 us
  waiting for transfers between devices  44.8 us (44%)
  starting transfers between devices  37 us (36%)
  Pallas kernels  13.7 us (13%)
  local copies, waits for them, and re-layouts  3.06 us (3%)
  other arithmetic  1.67 us (2%)
  between operations  1.43 us (1%)
    all_to_all x1, waiting for transfers between devices, per_device(): lax.all_to_all(outgoing, OPS, split_axis=0, concat_axis=0, tiled=True)  25.9 us
    ppermute x7, starting transfers between devices, own_share(): parts.append(lax.ppermute(block.astype(jnp.bfloat16), axes, hop))  14.3 us
    all_to_all x1, starting transfers between devices, gather_wave(): lax.all_to_all(jnp.broadcast_to(shard, (owners, *shard.shape)), OPS, 0, 0...  11.5 us
    all_to_all x1, waiting for transfers between devices, gather_wave(): lax.all_to_all(jnp.broadcast_to(shard, (owners, *shard.shape)), OPS, 0, 0...  9.58 us
    all_to_all x1, starting transfers between devices, per_device(): lax.all_to_all(outgoing, OPS, split_axis=0, concat_axis=0, tiled=True)  6.48 us
    ppermute x7, waiting for transfers between devices, own_share(): parts.append(lax.ppermute(block.astype(jnp.bfloat16), axes, hop))  5.83 us
    pallas_call x1, Pallas kernels, apply_pairs(): pl.pallas_call(sigma_kernel, in_specs=[smem, smem, vmem, hbm, hbm], out_s...  5.42 us
    pallas_call x2, Pallas kernels, rotate_left(): pl.pallas_call(functools.partial(rotate_kernel, start), in_specs=[pl.Bloc...  4.11 us
  transfers between devices with their start and end apart: 13, of which 6 were waited for; matrix products, arithmetic and copies ran while one was open for 2% of the time, Pallas kernels for 7%

profile of v3, /device:TPU:0, one launch (start us, length us, event | category | flops | bytes accessed | tf_op | source)
XLA Modules:
  0.0 101.6 jit_solution(17827556739760284124)
XLA Ops:
  0.6 1.4 %broadcast_in_dim.8 = bf16[64,3,4,128]{3,2,1,0:T(4,128)(2,1)} broadcast(bf16[3,4,128]{2,1,0:T(4,128)(2,1)} %bitcast.53), dimensions={1,2,3} | broadcast | bytes 199680 | tf_op jit(solution)/shard_map/broadcast_in_dim | solution.py:282
  2.0 11.5 %all-to-all-start = ((bf16[64,3,4,128]{3,2,1,0:T(4,128)(2,1)}), bf16[64,3,4,128]{3,2,1,0:T(4,128)(2,1)S(1)}, u32[]{:S(2)}, u32[]{:S(2)}) async-start(bf16[64,3,4,128]{3,2,1,0:T(4,128)(2,1)} %broadcast_in_dim.8), calls=%async_computation | async-start | bytes 393216 | tf_op jit(solution)/shard_map/all_to_all | solution.py:281
  14.2 9.6 %all-to-all-done = bf16[64,3,4,128]{3,2,1,0:T(4,128)(2,1)S(1)} async-done(((bf16[64,3,4,128]{3,2,1,0:T(4,128)(2,1)}), bf16[64,3,4,128]{3,2,1,0:T(4,128)(2,1)S(1)}, u32[]{:S(2)}, u32[]{:S(2)}) %all-to-all-start) | async-done | bytes 196640 | tf_op jit(solution)/shard_map/all_to_all | solution.py:281
  23.8 0.1 copy.14
  24.0 0.1 copy.15.wave_ref
  24.1 0.0 copy-start
  24.1 5.4 %apply_pairs.1 = (f32[8,2,8,768]{3,2,1,0:T(8,128)S(1)}, bf16[8,2,8,768]{3,2,1,0:T(8,128)(2,1)S(1)}) custom-call(s32[1]{0:T(128)} %bitcast.side_ref, s32[1]{0:T(128)S(6)} %copy.20.count_ref, bf16[384,256]{1,0:T(8,128)(2,1)S(1)} %copy.15.wave_ref, bf16[64,256,128]{2,1,0:T(8,128)(2,1)} %left_ref.5, bf16[64,256,256]{2,1,0:T(8,128)(2,1)} %right_ref.1), custom_call_target="tpu_custom_call" | custom-call | flops 6442450944 | bytes 12582912 | tf_op jit(solution)/shard_map/apply_pairs/pallas_call | solution.py:214
  29.5 0.1 collective-permute-start
  29.6 0.0 copy-done
  29.6 2.1 %rotate_left.3 = (bf16[32,64,128]{2,1,0:T(8,128)(2,1)S(1)}, bf16[32,64,128]{2,1,0:T(8,128)(2,1)S(1)}) custom-call(s32[1]{0:T(128)} %bitcast.side_ref, bf16[64,256,128]{2,1,0:T(8,128)(2,1)} %left_ref.5, bf16[256,128]{1,0:T(8,128)(2,1)S(1)} %copy-done), custom_call_target="tpu_custom_call" | custom-call | flops 268435456 | bytes 3145728 | tf_op jit(solution)/shard_map/rotate_left/pallas_call | solution.py:53
  31.7 0.6 collective-permute-start.9
  32.3 0.0 collective-permute-done
  32.3 0.0 copy-start.1
  32.4 0.7 copy-done.1
  33.1 0.0 copy-start.2
  33.1 1.7 %collective-permute-start.1 = (bf16[2,8,768]{2,1,0:T(8,128)(2,1)S(1)}, bf16[2,8,768]{2,1,0:T(8,128)(2,1)S(1)}, u32[]{:S(2)}, u32[]{:S(2)}) collective-permute-start(bf16[2,8,768]{2,1,0:T(8,128)(2,1)S(1)} %get-tuple-element.14), channel_id=1, source_target_pairs={{0,2},{2,4},{4,6},{6,0},{16,18},{18,20},{20,22},{22,16},{1,3},{3,5... | collective-permute-start | bytes 73736 | tf_op jit(solution)/shard_map/ppermute | solution.py:270
  34.8 2.1 %rotate_left.2 = (bf16[32,64,128]{2,1,0:T(8,128)(2,1)S(1)}, bf16[32,64,128]{2,1,0:T(8,128)(2,1)S(1)}) custom-call(s32[1]{0:T(128)} %bitcast.side_ref, bf16[64,256,128]{2,1,0:T(8,128)(2,1)} %left_ref.5, bf16[256,128]{1,0:T(8,128)(2,1)S(1)} %copy-done), custom_call_target="tpu_custom_call" | custom-call | flops 268435456 | bytes 3145728 | tf_op jit(solution)/shard_map/rotate_left/pallas_call | solution.py:53
  36.8 0.1 collective-permute-start.8
  36.9 5.3 %collective-permute-start.7 = (bf16[2,8,768]{2,1,0:T(8,128)(2,1)S(1)}, bf16[2,8,768]{2,1,0:T(8,128)(2,1)S(1)}, u32[]{:S(2)}, u32[]{:S(2)}) collective-permute-start(bf16[2,8,768]{2,1,0:T(8,128)(2,1)S(1)} %get-tuple-element.15), channel_id=1, source_target_pairs={{0,22},{2,16},{4,18},{6,20},{16,6},{18,0},{20,2},{22,4},{1,23},{3,... | collective-permute-start | bytes 73736 | tf_op jit(solution)/shard_map/ppermute | solution.py:270
  42.2 0.0 collective-permute-start.6
  42.2 0.0 collective-permute-done.1
  42.2 3.5 %collective-permute-start.5 = (bf16[2,8,768]{2,1,0:T(8,128)(2,1)S(1)}, bf16[2,8,768]{2,1,0:T(8,128)(2,1)S(1)}, u32[]{:S(2)}, u32[]{:S(2)}) collective-permute-start(bf16[2,8,768]{2,1,0:T(8,128)(2,1)S(1)} %get-tuple-element.17), channel_id=1, source_target_pairs={{0,18},{2,20},{4,22},{6,16},{16,2},{18,4},{20,6},{22,0},{1,19},{3,... | collective-permute-start | bytes 73736 | tf_op jit(solution)/shard_map/ppermute | solution.py:270
  45.8 0.0 copy-done.2
  45.8 0.2 convert_reduce_fusion.1
  45.9 0.0 collective-permute-done.7
  46.0 2.1 %collective-permute-start.4 = (bf16[2,8,768]{2,1,0:T(8,128)(2,1)S(1)}, bf16[2,8,768]{2,1,0:T(8,128)(2,1)S(1)}, u32[]{:S(2)}, u32[]{:S(2)}) collective-permute-start(bf16[2,8,768]{2,1,0:T(8,128)(2,1)S(1)} %get-tuple-element.18), channel_id=1, source_target_pairs={{0,16},{2,18},{4,20},{6,22},{16,0},{18,2},{20,4},{22,6},{1,17},{3,... | collective-permute-start | bytes 73736 | tf_op jit(solution)/shard_map/ppermute | solution.py:270
  48.0 2.0 %collective-permute-done.6 = bf16[2,8,768]{2,1,0:T(8,128)(2,1)S(1)} collective-permute-done((bf16[2,8,768]{2,1,0:T(8,128)(2,1)S(1)}, bf16[2,8,768]{2,1,0:T(8,128)(2,1)S(1)}, u32[]{:S(2)}, u32[]{:S(2)}) %collective-permute-start.6) | collective-permute-done | bytes 24608 | tf_op jit(solution)/shard_map/ppermute | solution.py:270
  50.0 0.3 collective-permute-start.3
  50.2 0.0 collective-permute-done.5
  50.2 1.5 %collective-permute-start.2 = (bf16[2,8,768]{2,1,0:T(8,128)(2,1)S(1)}, bf16[2,8,768]{2,1,0:T(8,128)(2,1)S(1)}, u32[]{:S(2)}, u32[]{:S(2)}) collective-permute-start(bf16[2,8,768]{2,1,0:T(8,128)(2,1)S(1)} %get-tuple-element.20), channel_id=1, source_target_pairs={{0,4},{2,6},{4,0},{6,2},{16,20},{18,22},{20,16},{22,18},{1,5},{3,7... | collective-permute-start | bytes 73736 | tf_op jit(solution)/shard_map/ppermute | solution.py:270
  51.7 0.0 collective-permute-done.4
  51.7 2.1 %collective-permute-done.3 = bf16[2,8,768]{2,1,0:T(8,128)(2,1)S(1)} collective-permute-done((bf16[2,8,768]{2,1,0:T(8,128)(2,1)S(1)}, bf16[2,8,768]{2,1,0:T(8,128)(2,1)S(1)}, u32[]{:S(2)}, u32[]{:S(2)}) %collective-permute-start.3) | collective-permute-done | bytes 24608 | tf_op jit(solution)/shard_map/ppermute | solution.py:270
  53.8 1.8 %collective-permute-done.2 = bf16[2,8,768]{2,1,0:T(8,128)(2,1)S(1)} collective-permute-done((bf16[2,8,768]{2,1,0:T(8,128)(2,1)S(1)}, bf16[2,8,768]{2,1,0:T(8,128)(2,1)S(1)}, u32[]{:S(2)}, u32[]{:S(2)}) %collective-permute-start.2) | collective-permute-done | bytes 24608 | tf_op jit(solution)/shard_map/ppermute | solution.py:270
  55.6 0.8 fusion.15
  56.4 0.6 copy.16
  57.0 4.0 %all-to-all-start.1 = ((bf16[8,2,768]{2,1,0:T(2,128)(2,1)}), bf16[8,2,768]{2,1,0:T(2,128)(2,1)S(1)}, u32[]{:S(2)}, u32[]{:S(2)}) async-start(bf16[8,2,768]{2,1,0:T(2,128)(2,1)} %copy.16), calls=%async_computation.1 | async-start | bytes 49152 | tf_op jit(solution)/shard_map/all_to_all | solution.py:311
  61.0 0.0 collective-permute-done.9.refs_3_
  61.0 0.0 collective-permute-done.8.refs_2_
  61.0 2.8 %renew.1 = bf16[128,64,128]{2,1,0:T(8,128)(2,1)} custom-call(s32[1]{0:T(128)} %bitcast.side_ref, s32[1]{0:T(128)S(6)} %copy.20.count_ref, s32[64]{0:T(128)S(1)} %multiply_add_fusion.place_ref, bf16[256,128]{1,0:T(8,128)(2,1)S(1)} %copy-done, bf16[32,64,128]{2,1,0:T(8,128)(2,1)S(1)} %get-tuple-element.10.refs_0_, ...), custom_call_target="tpu_custom_call" | custom-call | flops 268435456 | bytes 4194304 | tf_op jit(solution)/shard_map/renew/pallas_call | solution.py:109
  63.8 3.4 %all-to-all-done.1 = bf16[8,2,768]{2,1,0:T(2,128)(2,1)S(1)} async-done(((bf16[8,2,768]{2,1,0:T(2,128)(2,1)}), bf16[8,2,768]{2,1,0:T(2,128)(2,1)S(1)}, u32[]{:S(2)}, u32[]{:S(2)}) %all-to-all-start.1) | async-done | bytes 24608 | tf_op jit(solution)/shard_map/all_to_all | solution.py:311
  67.2 6.5 %all-to-all-start.2 = ((bf16[128,64,128]{2,1,0:T(8,128)(2,1)}), bf16[128,64,128]{2,1,0:T(8,128)(2,1)S(1)}, u32[]{:S(2)}, u32[]{:S(2)}) async-start(bf16[128,64,128]{2,1,0:T(8,128)(2,1)} %renew.1), calls=%async_computation.2 | async-start | bytes 4194304 | tf_op jit(solution)/shard_map/all_to_all | solution.py:306
  73.7 0.6 convert_reduce_fusion
  74.3 25.9 %all-to-all-done.2.in_ref = bf16[128,64,128]{2,1,0:T(8,128)(2,1)S(1)} async-done(((bf16[128,64,128]{2,1,0:T(8,128)(2,1)}), bf16[128,64,128]{2,1,0:T(8,128)(2,1)S(1)}, u32[]{:S(2)}, u32[]{:S(2)}) %all-to-all-start.2) | async-done | bytes 2097184 | tf_op jit(solution)/shard_map/all_to_all | solution.py:306
  100.3 1.3 %store.1 = bf16[128,64,128]{2,1,0:T(8,128)(2,1)} custom-call(bf16[128,64,128]{2,1,0:T(8,128)(2,1)S(1)} %all-to-all-done.2.in_ref), custom_call_target="tpu_custom_call" | custom-call | flops 4194304 | bytes 4194304 | tf_op jit(solution)/shard_map/store/pallas_call | solution.py:245
  (4 shorter events, 0.1 us)
Async XLA Ops:
  2.0 21.8 %all-to-all-start = ((bf16[64,3,4,128]{3,2,1,0:T(4,128)(2,1)}), bf16[64,3,4,128]{3,2,1,0:T(4,128)(2,1)S(1)}, u32[]{:S(2)}, u32[]{:S(2)}) async-start(bf16[64,3,4,128]{3,2,1,0:T(4,128)(2,1)} %broadcast_in_dim.8), calls=%async_computation | async-start | bytes 393216 | tf_op jit(solution)/shard_map/all_to_all | solution.py:281
  24.1 5.5 %copy-start = (bf16[256,128]{1,0:T(8,128)(2,1)S(1)}, bf16[256,128]{1,0:T(8,128)(2,1)}, u32[]{:S(2)}) copy-start(bf16[256,128]{1,0:T(8,128)(2,1)} %rot_ref.5) | copy-start | bytes 196612
  29.5 2.7 %collective-permute-start = (bf16[8,2,8,768]{3,2,1,0:T(8,128)(2,1)S(1)}, bf16[8,2,8,768]{3,2,1,0:T(8,128)(2,1)S(1)}, u32[]{:S(2)}, u32[]{:S(2)}) collective-permute-start(bf16[8,2,8,768]{3,2,1,0:T(8,128)(2,1)S(1)} %get-tuple-element.9), channel_id=1, source_target_pairs={{0,1},{1,0},{2,3},{3,2},{4,5},{5,4},{6,7},{7,6},{8,9},{9,8},{10,11... | collective-permute-start | bytes 589832 | tf_op jit(solution)/shard_map/ppermute | solution.py:308
  31.7 29.3 %collective-permute-start.9 = (bf16[32,64,128]{2,1,0:T(8,128)(2,1)S(1)}, bf16[32,64,128]{2,1,0:T(8,128)(2,1)S(1)}, u32[]{:S(2)}, u32[]{:S(2)}) collective-permute-start(bf16[32,64,128]{2,1,0:T(8,128)(2,1)S(1)} %get-tuple-element.13), channel_id=1, source_target_pairs={{0,1},{1,0},{2,3},{3,2},{4,5},{5,4},{6,7},{7,6},{8,9},{9,8},{10,11... | collective-permute-start | bytes 1572872 | tf_op jit(solution)/shard_map/ppermute | solution.py:302
  32.3 0.7 copy-start.1
  33.1 12.7 %copy-start.2 = (s32[64,1]{0,1:T(1,128)S(1)}, s32[64,1]{0,1:T(1,128)}, u32[]{:S(2)}) copy-start(s32[64,1]{0,1:T(1,128)} %param.11) | copy-start | bytes 772
  33.1 9.2 %collective-permute-start.1 = (bf16[2,8,768]{2,1,0:T(8,128)(2,1)S(1)}, bf16[2,8,768]{2,1,0:T(8,128)(2,1)S(1)}, u32[]{:S(2)}, u32[]{:S(2)}) collective-permute-start(bf16[2,8,768]{2,1,0:T(8,128)(2,1)S(1)} %get-tuple-element.14), channel_id=1, source_target_pairs={{0,2},{2,4},{4,6},{6,0},{16,18},{18,20},{20,22},{22,16},{1,3},{3,5... | collective-permute-start | bytes 73736 | tf_op jit(solution)/shard_map/ppermute | solution.py:270
  36.8 24.2 %collective-permute-start.8 = (bf16[32,64,128]{2,1,0:T(8,128)(2,1)S(1)}, bf16[32,64,128]{2,1,0:T(8,128)(2,1)S(1)}, u32[]{:S(2)}, u32[]{:S(2)}) collective-permute-start(bf16[32,64,128]{2,1,0:T(8,128)(2,1)S(1)} %get-tuple-element.12), channel_id=1, source_target_pairs={{0,1},{1,0},{2,3},{3,2},{4,5},{5,4},{6,7},{7,6},{8,9},{9,8},{10,11... | collective-permute-start | bytes 1572872 | tf_op jit(solution)/shard_map/ppermute | solution.py:302
  36.9 9.0 %collective-permute-start.7 = (bf16[2,8,768]{2,1,0:T(8,128)(2,1)S(1)}, bf16[2,8,768]{2,1,0:T(8,128)(2,1)S(1)}, u32[]{:S(2)}, u32[]{:S(2)}) collective-permute-start(bf16[2,8,768]{2,1,0:T(8,128)(2,1)S(1)} %get-tuple-element.15), channel_id=1, source_target_pairs={{0,22},{2,16},{4,18},{6,20},{16,6},{18,0},{20,2},{22,4},{1,23},{3,... | collective-permute-start | bytes 73736 | tf_op jit(solution)/shard_map/ppermute | solution.py:270
  42.2 7.7 %collective-permute-start.6 = (bf16[2,8,768]{2,1,0:T(8,128)(2,1)S(1)}, bf16[2,8,768]{2,1,0:T(8,128)(2,1)S(1)}, u32[]{:S(2)}, u32[]{:S(2)}) collective-permute-start(bf16[2,8,768]{2,1,0:T(8,128)(2,1)S(1)} %get-tuple-element.16), channel_id=1, source_target_pairs={{0,20},{2,22},{4,16},{6,18},{16,4},{18,6},{20,0},{22,2},{1,21},{3,... | collective-permute-start | bytes 73736 | tf_op jit(solution)/shard_map/ppermute | solution.py:270
  42.2 8.0 %collective-permute-start.5 = (bf16[2,8,768]{2,1,0:T(8,128)(2,1)S(1)}, bf16[2,8,768]{2,1,0:T(8,128)(2,1)S(1)}, u32[]{:S(2)}, u32[]{:S(2)}) collective-permute-start(bf16[2,8,768]{2,1,0:T(8,128)(2,1)S(1)} %get-tuple-element.17), channel_id=1, source_target_pairs={{0,18},{2,20},{4,22},{6,16},{16,2},{18,4},{20,6},{22,0},{1,19},{3,... | collective-permute-start | bytes 73736 | tf_op jit(solution)/shard_map/ppermute | solution.py:270
  46.0 5.8 %collective-permute-start.4 = (bf16[2,8,768]{2,1,0:T(8,128)(2,1)S(1)}, bf16[2,8,768]{2,1,0:T(8,128)(2,1)S(1)}, u32[]{:S(2)}, u32[]{:S(2)}) collective-permute-start(bf16[2,8,768]{2,1,0:T(8,128)(2,1)S(1)} %get-tuple-element.18), channel_id=1, source_target_pairs={{0,16},{2,18},{4,20},{6,22},{16,0},{18,2},{20,4},{22,6},{1,17},{3,... | collective-permute-start | bytes 73736 | tf_op jit(solution)/shard_map/ppermute | solution.py:270
  50.0 3.8 %collective-permute-start.3 = (bf16[2,8,768]{2,1,0:T(8,128)(2,1)S(1)}, bf16[2,8,768]{2,1,0:T(8,128)(2,1)S(1)}, u32[]{:S(2)}, u32[]{:S(2)}) collective-permute-start(bf16[2,8,768]{2,1,0:T(8,128)(2,1)S(1)} %get-tuple-element.19), channel_id=1, source_target_pairs={{0,6},{2,0},{4,2},{6,4},{16,22},{18,16},{20,18},{22,20},{1,7},{3,1... | collective-permute-start | bytes 73736 | tf_op jit(solution)/shard_map/ppermute | solution.py:270
  50.2 5.3 %collective-permute-start.2 = (bf16[2,8,768]{2,1,0:T(8,128)(2,1)S(1)}, bf16[2,8,768]{2,1,0:T(8,128)(2,1)S(1)}, u32[]{:S(2)}, u32[]{:S(2)}) collective-permute-start(bf16[2,8,768]{2,1,0:T(8,128)(2,1)S(1)} %get-tuple-element.20), channel_id=1, source_target_pairs={{0,4},{2,6},{4,0},{6,2},{16,20},{18,22},{20,16},{22,18},{1,5},{3,7... | collective-permute-start | bytes 73736 | tf_op jit(solution)/shard_map/ppermute | solution.py:270
  57.0 10.2 %all-to-all-start.1 = ((bf16[8,2,768]{2,1,0:T(2,128)(2,1)}), bf16[8,2,768]{2,1,0:T(2,128)(2,1)S(1)}, u32[]{:S(2)}, u32[]{:S(2)}) async-start(bf16[8,2,768]{2,1,0:T(2,128)(2,1)} %copy.16), calls=%async_computation.1 | async-start | bytes 49152 | tf_op jit(solution)/shard_map/all_to_all | solution.py:311
  67.2 33.0 %all-to-all-start.2 = ((bf16[128,64,128]{2,1,0:T(8,128)(2,1)}), bf16[128,64,128]{2,1,0:T(8,128)(2,1)S(1)}, u32[]{:S(2)}, u32[]{:S(2)}) async-start(bf16[128,64,128]{2,1,0:T(8,128)(2,1)} %renew.1), calls=%async_computation.2 | async-start | bytes 4194304 | tf_op jit(solution)/shard_map/all_to_all | solution.py:306
